TPU v7x, 32 devices: a whole 2x2x4 slice. The times are simulated.
32 devices in a mesh: row: 4 (over y, core), col: 4 (over z), layer: 2 (over x).
Axes of the slice: x: 2, y: 2, z: 4, core: 2. Of those that a mesh axis runs over, the one named last changes fastest.
Arguments:
- a_tiles: float32 [16, 2, 7, 128, 128], P(('row', 'col'), 'layer'), may hold values from -0.5 to 0.5
- a_cols: int32 [16, 2, 7], P(('row', 'col'), 'layer'), may hold values from -1 to 255, as said below
- b_tiles: float32 [256, 2, 7, 128, 128], P(('row', 'col'), 'layer'), may hold values from -6 to 6
- b_rows: int32 [256, 2, 7], P(('row', 'col'), 'layer'), may hold values from 0 to 255, as said below
- c_cols: int32 [16, 4, 4], P('row', 'col'), may hold values from 0 to 255, as said below
Outputs:
- c_tiles: float32 [16, 4, 4, 128, 128], P('row', 'col', 'layer')
Inputs may be any that keep to these rules, and one draw needn't show every extreme that they name: In a_cols[i, h, :] the used slots come first and hold distinct block columns in [h * 128, (h + 1) * 128); the unused ones hold -1. Some block rows use all 7 slots in each half, others few. b_rows[j, h, :] holds 7 distinct block rows in [h * 128, (h + 1) * 128). c_cols[i, g, :] holds 4 distinct block columns j with (j // 16) % 4 == g.
All inputs are finite; a program needn't handle non-finite values.
Results may differ from a plain program's by a relative error of at most 0.0003.
Values sent between devices are 32-bit elements; how exact they have to be, the bound alone decides.
No kernel may reach another device: no remote copies, remote signals or barrier semaphores. Data moves between devices by JAX's collectives and lax.ppermute only.
A program may use at most 128 MiB of HBM per device.

v0:
```python
import functools

import jax
import jax.numpy as jnp
import numpy as np
from jax import lax
from jax.experimental import pallas as pl
from jax.experimental.pallas import tpu as pltpu
from jax.sharding import PartitionSpec as P


AXES = ("row", "col", "layer")
SMEM = pltpu.SMEM
VMEM = pltpu.VMEM
HBM = pltpu.HBM
I32 = jnp.int32
F32 = jnp.float32
BF16 = jnp.bfloat16


def index_kernel(d, b_rows, a_cols, c_cols, out):
    for w in range(d.W):
        for s in range(d.S):
            out[0, w * d.S + s] = b_rows[s, 0, w]
    for r in range(d.AR):
        for s in range(d.SA):
            out[0, d.NB + r * d.SA + s] = a_cols[r, 0, s]
    for r in range(d.RPD):
        for q in range(d.Q):
            out[0, d.OFF_C + r * d.Q + q] = c_cols[r, 0, q]


def over(x, n):
    return jnp.floor((x.astype(F32) + 0.5) * (1.0 / n)).astype(I32)


def plan_kernel(d, me, gs, gv, inv_ref, cnt_ref, pos_ref, lvl_ref, need, need_send):
    b = gv[:, : d.NB]
    dev = lax.broadcasted_iota(I32, b.shape, 0)
    block = over(dev, d.L)
    lay_of = dev - block * d.L
    col_of = block * d.W + over(lax.broadcasted_iota(I32, b.shape, 1), d.S)
    tri_shape = (d.NB, d.NB)
    tri = jnp.where(
        lax.broadcasted_iota(I32, tri_shape, 0) <= lax.broadcasted_iota(I32, tri_shape, 1), 1.0, 0.0
    )
    most, most_send = jnp.int32(0), jnp.int32(0)

    def per_chip(x):
        return jnp.sum(jnp.sum(x.astype(F32).reshape(d.Y, d.PAIR, d.G * d.L, d.NB), axis=1), axis=2)

    for dst in range(d.Y):

        def one_row(i, acc):
            r = dst * d.PAIR + i // d.RPD
            ci = i % d.RPD
            wanted, wanted_send = None, None
            for h in range(d.L):
                part = None
                for g in range(d.G):
                    for q in range(h * d.QL, (h + 1) * d.QL):
                        hit = col_of == gs[(r * d.G + g) * d.L, d.OFF_C + ci * d.Q + q]
                        part = hit if part is None else part | hit
                away = part & (lay_of != h)
                wanted = part if wanted is None else wanted | part
                wanted_send = away if wanted_send is None else wanted_send | away
            match = None
            base = (r * d.G + ci // d.AR) * d.L
            for s in range(d.SA):
                at = d.NB + (ci % d.AR) * d.SA + s
                want = jnp.full(b.shape, gs[base, at], I32)
                for l in range(1, d.L):
                    want = jnp.where(lay_of == l, gs[base + l, at], want)
                hit = b == want
                match = hit if match is None else match | hit
            return (
                jnp.where(wanted & match, 1, acc[0]),
                jnp.where(wanted_send & match, 1, acc[1]),
            )

        zero = jnp.zeros(b.shape, I32)
        acc, send = lax.fori_loop(0, d.PAIR * d.RPD, one_row, (zero, zero))
        need[dst] = acc
        need_send[dst] = send
        chip = lax.broadcasted_iota(I32, (d.Y, d.G * d.L), 0)
        away = chip != dst
        most = jnp.maximum(most, jnp.max(jnp.where(away, per_chip(acc), 0.0)).astype(I32))
        most_send = jnp.maximum(most_send, jnp.max(jnp.where(away, per_chip(send), 0.0)).astype(I32))
    share = (most + d.PAIR - 1) // d.PAIR
    share_send = (most_send + d.PAIR - 1) // d.PAIR
    level = jnp.int32(0)
    for first, cap in d.caps[:-1]:
        level = level + ((share > cap) | (share_send > first)).astype(I32)
    lvl_ref[0] = level

    y = me[0] // d.PAIR
    mine = me[1] * d.L + me[2]
    lanes = lax.broadcasted_iota(I32, (d.NB, d.PAIR * d.NB), 1).astype(F32)
    ones = jnp.ones((8, d.NB), F32)

    def rows_of(ref, dst, src, c):
        return ref[dst, pl.ds((src * d.PAIR + c) * d.G * d.L + mine, 1), :].astype(F32)

    for delta in range(1, d.Y):
        dst = (y + delta) % d.Y
        src = (y + d.Y - delta) % d.Y
        for kind in range(2):
            before = jnp.float32(0)
            inv = jnp.zeros((1, d.PAIR * d.NB), F32)
            for c in range(d.PAIR):
                bits = rows_of(need_send, dst, y, c)
                if kind == 1:
                    bits = rows_of(need, dst, y, c) - bits
                wide = ones * bits
                upto = lax.dot_general(tri, wide, (((0,), (1,)), ((), ())), preferred_element_type=F32)
                inv = inv + jnp.sum(
                    jnp.where(upto[:, :1] + before <= lanes, 1.0, 0.0), axis=0, keepdims=True
                )
                before = before + jnp.sum(bits)
            inv_ref[delta - 1, kind : kind + 1, :] = inv.astype(I32)
            cnt_ref[delta - 1, kind] = before.astype(I32)
        before = jnp.float32(0)
        position = [None] * d.PAIR
        for kind in range(2):
            for c in range(d.PAIR):
                bits = rows_of(need_send, y, src, c)
                if kind == 1:
                    bits = rows_of(need, y, src, c) - bits
                ahead = jnp.dot(ones * bits, tri, preferred_element_type=F32)[:1] - bits + before
                position[c] = ahead if kind == 0 else jnp.where(bits > 0.5, ahead, position[c])
                before = before + jnp.sum(bits)
        for c in range(d.PAIR):
            pos_ref[delta - 1, c : c + 1, :] = position[c].astype(I32)


def pack_kernel(d, first, cap, me, inv, cnt, own, sib, out, out2, sem):
    core = me[0] % d.PAIR
    total = jnp.int32(0)
    for delta in range(d.Y - 1):
        send = cnt[delta, 0]
        count = (send + cnt[delta, 1] - core + d.PAIR - 1) // d.PAIR

        def one(k, _):
            p = k * d.PAIR + core
            late = jnp.maximum(p - send, 0)
            t = jnp.where(p < send, inv[delta, 0, p], inv[delta, 1, late])
            c = t // d.NB
            t = t % d.NB

            def put(dst):
                @pl.when(c == core)
                def _():
                    pltpu.make_async_copy(own.at[t], dst, sem).start()

                @pl.when(c != core)
                def _():
                    pltpu.make_async_copy(sib.at[t], dst, sem).start()

            @pl.when(k < first)
            def _():
                put(out.at[delta, jnp.minimum(k, first - 1)])

            if cap > first:

                @pl.when(k >= first)
                def _():
                    put(out2.at[delta, jnp.clip(k - first, 0, cap - first - 1)])

            return 0

        lax.fori_loop(0, count, one, 0)
        total = total + count

    def wait(k, _):
        pltpu.make_async_copy(own.at[0], out.at[0, 0], sem).wait()
        return 0

    lax.fori_loop(0, total, wait, 0)


def list_kernel(d, first_cap, me, gs, pos, src_ref, aidx_ref, oidx_ref, starts_ref):
    row, col, lay = me[0], me[1], me[2]
    y = row // d.PAIR
    n = jnp.int32(0)
    for k, (step, low, high, part) in enumerate(d.sections):
        starts_ref[k] = n
        half = (lay + step) % d.L

        def one_pair(i, n):
            sl_d = i // (d.AR * d.QL)
            ar = i // d.QL % d.AR
            qq = i % d.QL
            cc = (col + d.G - (low + sl_d)) % d.G
            ci = cc * d.AR + ar
            j = gs[(row * d.G + col) * d.L + lay, d.OFF_C + ci * d.Q + half * d.QL + qq]
            rp = j // (d.G * d.W)
            w = j % d.W
            a_dev = (row * d.G + cc) * d.L + lay
            a_vals = [gs[a_dev, d.NB + ar * d.SA + s] for s in range(d.SA)]
            a_base = (sl_d * d.AR + ar) * d.SA
            delta = (y + d.Y - rp // d.PAIR) % d.Y
            here = jnp.where(rp == row, 0, d.NB)

            def one_slot(sl, n):
                tile = w * d.S + sl
                b = gs[(rp * d.G + col) * d.L + lay, tile]
                s_hit = jnp.int32(-1)
                for s in range(d.SA):
                    s_hit = jnp.where(b == a_vals[s], s, s_hit)
                there = pos[jnp.maximum(delta - 1, 0), rp % d.PAIR, tile]
                take = s_hit >= 0
                if part is not None:
                    late = (delta != 0) & (there // d.PAIR >= first_cap)
                    take = take & (late == (part == 1))

                @pl.when(take)
                def _():
                    src_ref[n] = jnp.where(delta == 0, here + tile, 2 * d.NB * delta + there)
                    aidx_ref[n] = a_base + s_hit
                    oidx_ref[n] = i

                return n + take.astype(I32)

            return lax.fori_loop(0, d.S, one_slot, n)

        n = lax.fori_loop(0, (high - low) * d.AR * d.QL, one_pair, n)
    starts_ref[len(d.sections)] = n


def product_kernel(d, section, depth, first_cap, n_a, n_x, me, src, aidx, oidx, starts, *refs):
    last = n_x > 0
    n_local = 0 if last else 2
    local, (straight, crossed) = refs[:n_local], refs[n_local : n_local + 2]
    refs = refs[n_local + 2 :]
    a_refs, parts, out = refs[:n_a], refs[n_a : n_a + n_x], refs[n_a + n_x]
    a_all, buf, sem = refs[n_a + n_x + 1 :]
    core = me[0] % d.PAIR
    first = starts[section]
    n = starts[section + 1] - first
    base = first_cap if last else 0
    size = d.AR * d.QL

    def start(k):
        s = src[first + k]
        dst = buf.at[k % depth]
        done = sem.at[k % depth]
        if not last:

            @pl.when(s < d.NB)
            def _():
                pltpu.make_async_copy(local[0].at[jnp.minimum(s, d.NB - 1)], dst, done).start()

            @pl.when((s >= d.NB) & (s < 2 * d.NB))
            def _():
                pltpu.make_async_copy(local[1].at[jnp.clip(s - d.NB, 0, d.NB - 1)], dst, done).start()

        @pl.when(s >= 2 * d.NB)
        def _():
            rest = s - 2 * d.NB
            delta = jnp.minimum(rest // (2 * d.NB), straight.shape[0] - 1)
            p = rest % (2 * d.NB)
            at = jnp.clip(p // d.PAIR - base, 0, straight.shape[1] - 1)

            @pl.when(p % d.PAIR == core)
            def _():
                buf[k % depth] = straight[delta, at]

            @pl.when(p % d.PAIR != core)
            def _():
                buf[k % depth] = crossed[delta, at]

    def start_one(k, _):
        start(k)
        return 0

    lax.fori_loop(0, jnp.minimum(n, depth), start_one, 0)
    rows = d.AR * d.SA
    T = d.T

    @pl.when(n > 0)
    def _():
        for k in range(n_a):
            a = a_refs[k][...]
            hi = a.astype(BF16)
            a_all[k * rows : (k + 1) * rows, :T, :] = hi
            a_all[k * rows : (k + 1) * rows, T:, :] = (a - hi.astype(F32)).astype(BF16)

    def place(slot):
        return (me[1] + d.G - slot) % d.G * size

    if last:
        for k in range(d.G):
            total = parts[0][k * size : (k + 1) * size]
            for m in range((n_x - 1) // 2):
                early, late = parts[1 + 2 * m], parts[2 + 2 * m]
                total = total + (
                    early[k * size : (k + 1) * size]
                    if k < d.EARLY
                    else late[(k - d.EARLY) * size : (k - d.EARLY + 1) * size]
                )
            out[pl.ds(place(k), size)] = total
    else:
        out[...] = jnp.zeros(out.shape, out.dtype)

    def product(k, valid):
        if not last:

            @pl.when(valid & (src[first + k] < 2 * d.NB))
            def _():
                pltpu.make_async_copy(local[0].at[0], buf.at[k % depth], sem.at[k % depth]).wait()

        b = buf[k % depth]
        b = jnp.where(valid, b, 0.0)
        b_hi = b.astype(BF16)
        b_lo = (b - b_hi.astype(F32)).astype(BF16)
        a = a_all[aidx[first + k]]
        both = jnp.dot(a, b_hi, preferred_element_type=F32)
        low = jnp.dot(a[:T], b_lo, preferred_element_type=F32)
        return both[:T] + (both[T:] + low)

    def add(k, value):
        o = oidx[first + k]
        if last:
            o = place(o // size) + o % size
        out[o] = out[o] + value

    def two(i, _):
        k = 2 * i
        valid = k + 1 < n
        k1 = jnp.minimum(k + 1, n - 1)
        p0 = product(k, k < n)
        p1 = product(k1, valid)
        add(k, p0)
        add(k1, p1)
        lax.fori_loop(jnp.minimum(k + depth, n), jnp.minimum(k + depth + 2, n), start_one, 0)
        return 0

    lax.fori_loop(0, (n + 1) // 2, two, 0)


class Dims:
    pass


def on_device(a_tiles, a_cols, b_tiles, b_rows, c_cols):
    d = Dims()
    d.R, d.G, d.L = (lax.axis_size(name) for name in AXES)
    d.W, d.S, d.T = b_tiles.shape[0], b_tiles.shape[2], b_tiles.shape[-1]
    d.AR, d.SA = a_tiles.shape[0], a_tiles.shape[2]
    d.RPD, d.Q = c_cols.shape[0], c_cols.shape[2]
    d.PAIR = 2 if d.R % 2 == 0 else 1
    d.Y, d.NB, d.N, d.QL = d.R // d.PAIR, d.W * d.S, d.R * d.G * d.L, d.Q // d.L
    d.OFF_C = d.NB + d.AR * d.SA
    d.EARLY = 1 + max(1, d.G // 4)
    totals = sorted({-(-d.NB * k // 56) for k in (8, 9, 10, 11, 12, 14, 18, 28)})
    d.caps = tuple((-(-t * 5 // 8), t) for t in totals) + ((d.NB, d.NB),)
    d.sections = tuple(
        (step, low, high, None)
        for step in range(1, d.L)
        for low, high in ((0, d.EARLY), (d.EARLY, d.G))
    ) + ((0, 0, d.G, 0), (0, 0, d.G, 1))
    R, G, L, T, NB, PAIR, Y = d.R, d.G, d.L, d.T, d.NB, d.PAIR, d.Y
    YS = max(Y - 1, 1)
    smem = pl.BlockSpec(memory_space=SMEM)
    vmem = pl.BlockSpec(memory_space=VMEM)
    hbm = pl.BlockSpec(memory_space=HBM)

    def shift(x, k):
        return lax.ppermute(x, "col", [(c, (c + k) % G) for c in range(G)])

    own = b_tiles.reshape(NB, T, T)
    pair_swap = [(r, r ^ (PAIR - 1)) for r in range(R)]
    a_own = a_tiles.reshape(d.AR * d.SA, T, T)
    me = jnp.stack([lax.axis_index(name) for name in AXES]).astype(I32)
    n_idx = d.OFF_C + d.RPD * d.Q

    def limit(*shapes):
        return pltpu.CompilerParams(
            vmem_limit_bytes=(2 << 20) + sum(4 * int(np.prod(shape)) for shape in shapes)
        )

    idx = pl.pallas_call(
        functools.partial(index_kernel, d),
        in_specs=[smem] * 3,
        out_specs=smem,
        out_shape=jax.ShapeDtypeStruct((1, n_idx), I32),
        compiler_params=limit(),
        name="index",
    )(b_rows.transpose(2, 1, 0), a_cols, c_cols)
    group = lax.all_gather(idx, "col", axis=0, tiled=True)
    sib = lax.ppermute(own, "row", pair_swap)
    a_from, group = lax.optimization_barrier((a_own, group))
    a_early = [a_own] + [shift(a_from, k) for k in range(1, d.EARLY)]
    table = lax.all_to_all(
        jnp.broadcast_to(group[None], (R * L, G, n_idx)), ("row", "layer"), 0, 0, tiled=True
    )
    table = table.reshape(R, L, G, n_idx).transpose(0, 2, 1, 3).reshape(d.N, n_idx)

    inv, cnt, pos, level = pl.pallas_call(
        functools.partial(plan_kernel, d),
        in_specs=[smem, smem, vmem],
        out_specs=[vmem, smem, vmem, smem],
        out_shape=[
            jax.ShapeDtypeStruct((YS, 2, PAIR * NB), I32),
            jax.ShapeDtypeStruct((YS, 2), I32),
            jax.ShapeDtypeStruct((YS, PAIR, NB), I32),
            jax.ShapeDtypeStruct((1,), I32),
        ],
        scratch_shapes=[VMEM((Y, d.N, NB), I32)] * 2,
        compiler_params=limit((2 * Y + 8, d.N, 128), (16, 256, 256)),
        name="plan",
    )(me, table, table)

    most = d.RPD * d.Q * d.S

    def run(branch, me, table, inv, cnt, pos, own, sib, *a_early):
        return body(d.caps[branch], me, table, inv, cnt, pos, own, sib, *a_early)

    def body(caps, me, table, inv, cnt, pos, own, sib, *a_early):
        first, cap = caps
        two = cap > first
        second = max(cap - first, 1)
        a_late = [shift(a_early[0], k) for k in range(d.EARLY, G)]
        packs = pl.pallas_call(
            functools.partial(pack_kernel, d, first, cap),
            in_specs=[smem, smem, smem, hbm, hbm],
            out_specs=[vmem, vmem],
            out_shape=[
                jax.ShapeDtypeStruct((YS, first, T, T), F32),
                jax.ShapeDtypeStruct((YS, second, T, T), F32),
            ],
            scratch_shapes=[pltpu.SemaphoreType.DMA],
            compiler_params=limit((YS, first, T, T), (YS, second, T, T)),
            name="pack",
        )(me, inv, cnt, own, sib)

        def across(piece):
            packed = packs[piece]
            recs = [
                lax.ppermute(
                    packed[k - 1 : k],
                    "row",
                    [(r, ((r // PAIR + k) % Y) * PAIR + r % PAIR) for r in range(R)],
                )
                for k in range(1, Y)
            ]
            rec = recs[0] if len(recs) == 1 else jnp.concatenate(recs, 0)
            return [rec, lax.ppermute(rec, "row", pair_swap)]

        received = [across(0), across(1) if two else [packs[1], packs[1]]]
        a_list = list(a_early) + a_late
        src, aidx, oidx, starts = pl.pallas_call(
            functools.partial(list_kernel, d, first),
            in_specs=[smem, smem, smem],
            out_specs=[smem, smem, smem, smem],
            out_shape=[jax.ShapeDtypeStruct((most,), I32)] * 3
            + [jax.ShapeDtypeStruct((len(d.sections) + 1,), I32)],
            compiler_params=limit(),
            cost_estimate=pl.CostEstimate(flops=5 * 10**9, bytes_accessed=10**5, transcendentals=0),
            name="list",
        )(me, table, pos)

        depth = 8

        def products(k, parts=()):
            _, low, high, part = d.sections[k]
            b_local = [] if part == 1 else [own, sib]
            b_far = received[1 if part == 1 else 0]
            a_part = a_list[low:high]
            size = ((high - low) * d.AR * d.QL, T, T)
            n_a = len(a_part) * d.AR * d.SA
            return pl.pallas_call(
                functools.partial(product_kernel, d, k, depth, first, len(a_part), len(parts)),
                in_specs=[smem] * 5
                + [hbm] * len(b_local)
                + [vmem] * (2 + len(a_part) + len(parts)),
                out_specs=vmem,
                out_shape=jax.ShapeDtypeStruct(size, F32),
                scratch_shapes=[
                    VMEM((n_a, 2 * T, T), BF16),
                    VMEM((depth, T, T), F32),
                    pltpu.SemaphoreType.DMA((depth,)),
                ],
                compiler_params=limit(
                    (depth + 2 * n_a, T, T), size, *(x.shape for x in (*b_far, *parts))
                ),
                cost_estimate=pl.CostEstimate(
                    flops=5 * 10**9, bytes_accessed=10**6, transcendentals=0
                ),
                name="products",
            )(me, src, aidx, oidx, starts, *b_local, *b_far, *a_part, *parts)

        moved = []
        for k, (step, _, _, _) in enumerate(d.sections[:-2]):
            part = products(k)
            moved.append(lax.ppermute(part, "layer", [(l, (l + step) % L) for l in range(L)]))
        mine = products(len(d.sections) - 2)
        return products(len(d.sections) - 1, [mine, *moved])

    result = lax.switch(
        level[0],
        [functools.partial(run, k) for k in range(len(d.caps))],
        me, table, inv, cnt, pos, own, sib, *a_early,
    )
    return result.reshape(d.RPD, 1, d.QL, T, T)


def solution(mesh):
    return jax.shard_map(
        on_device,
        mesh=mesh,
        in_specs=(
            P(("row", "col"), "layer", None, None, None),
            P(("row", "col"), "layer", None),
            P(("row", "col"), "layer", None, None, None),
            P(("row", "col"), "layer", None),
            P("row", "col", None),
        ),
        out_specs=P("row", "col", "layer", None, None),
        check_vma=False,
    )
```

profile of v0, /device:TPU:29, one launch (start us, length us, event | category | flops | bytes accessed | tf_op | source)
XLA Modules:
  0.0 101.0 jit_solution(17610299453275656245)
XLA Ops:
  0.7 0.7 copy-done
  2.7 1.3 %index.1 = s32[1,135]{1,0:T(1,128)S(1)} custom-call(s32[7,1,16]{2,1,0:T(1,128)S(1)} %bitcast.42, s32[1,1,7]{2,1,0:T(1,128)S(1)} %copy-done.2, s32[4,1,4]{2,1,0:T(1,128)S(1)} %copy-done.1), custom_call_target="tpu_custom_call" | custom-call | tf_op jit(solution)/shard_map/index/pallas_call | solution.py:382
  4.0 5.6 %all-gather = s32[4,1,135]{2,1,0:T(1,128)S(1)} all-gather(s32[1,1,135]{2,1,0:T(1,128)S(1)} %bitcast.41), channel_id=1, replica_groups=mesh['row'=4,'col'=4,'layer'=2] {'col'}, dimensions={0}, use_global_device_ids=true | all-gather | bytes 2700 | tf_op jit(solution)/shard_map/all_gather | solution.py:390
  9.6 3.5 %collective-permute-start.71 = (f32[7,128,128]{2,1,0:T(8,128)}, f32[7,128,128]{2,1,0:T(8,128)S(1)}, u32[]{:S(2)}, u32[]{:S(2)}) collective-permute-start(f32[7,128,128]{2,1,0:T(8,128)} %bitcast.71), channel_id=1, source_target_pairs={{0,2},{2,4},{4,6},{6,0},{1,3},{3,5},{5,7},{7,1},{8,10},{10,12},{12... | collective-permute-start | bytes 1376264 | tf_op jit(solution)/shard_map/ppermute | solution.py:369
  13.7 6.1 %all-to-all-start = ((s32[8,4,135]{2,1,0:T(4,128)}), s32[8,4,135]{2,1,0:T(4,128)S(1)}, u32[]{:S(2)}, u32[]{:S(2)}) async-start(s32[8,4,135]{2,1,0:T(4,128)} %broadcast_in_dim.2), calls=%async_computation | async-start | bytes 65536 | tf_op jit(solution)/shard_map/all_to_all | solution.py:394
  19.9 3.2 %all-to-all-done = s32[8,4,135]{2,1,0:T(4,128)S(1)} async-done(((s32[8,4,135]{2,1,0:T(4,128)}), s32[8,4,135]{2,1,0:T(4,128)S(1)}, u32[]{:S(2)}, u32[]{:S(2)}) %all-to-all-start) | async-done | bytes 17312 | tf_op jit(solution)/shard_map/all_to_all | solution.py:394
  23.2 3.4 %plan.1 = (s32[1,2,224]{2,1,0:T(2,128)S(1)}, s32[1,2]{1,0:T(1,128)S(1)}, s32[1,2,112]{2,1,0:T(2,128)S(1)}, s32[1]{0:T(128)}) custom-call(s32[3]{0:T(128)S(1)} %pad_add_fusion.me, s32[32,135]{1,0:T(8,128)S(1)} %reshape.46.gs.gv, s32[32,135]{1,0:T(8,128)S(1)} %reshape.46.gs.gv), custom_call_target="tpu_custom_call" | custom-call | tf_op jit(solution)/shard_map/plan/pallas_call | solution.py:399
  27.3 73.0 %conditional.1 = (f32[4,1,2,128,128]{4,3,2,1,0:T(8,128)S(1)}) conditional(s32[]{:T(128)} %bitcast.35, (s32[3]{0:T(128)S(1)}, s32[32,135]{1,0:T(8,128)S(1)}, s32[1,2,112]{2,1,0:T(2,128)S(1)}, s32[1,2,224]{2,1,0:T(2,128)S(1)}, s32[1,2]{1,0:T(1,128)S(1)}, /*index=5*/f32[112,128,128]{2,1,0:T(8,128)}, ...), branch_computations={%region_0.0_spmd, %region_1.0_spmd, %region_2.0_spmd, %region_3.0_... | conditional | flops 24999999488 | bytes 92442856 | solution.py:500
  27.3 2.1 %pack.12 = (f32[1,14,128,128]{3,2,1,0:T(8,128)S(1)}, f32[1,8,128,128]{3,2,1,0:T(8,128)S(1)}) custom-call(s32[3]{0:T(128)S(1)} %get-tuple-element.223.me, s32[1,2,224]{2,1,0:T(2,128)S(1)} %get-tuple-element.230.inv, s32[1,2]{1,0:T(1,128)S(1)} %get-tuple-element.231.cnt, f32[112,128,128]{2,1,0:T(8,128)} %get-tuple-element.232.own.refs_0_, ...), custom_call_target="tpu_custom_call" | custom-call | tf_op jit(solution)/shard_map/cond/branch_3_fun/pack/pallas_call | solution.py:424
  29.5 1.4 %collective-permute-start.28 = (f32[1,14,128,128]{3,2,1,0:T(8,128)S(1)}, f32[1,14,128,128]{3,2,1,0:T(8,128)S(1)}, u32[]{:S(2)}, u32[]{:S(2)}) collective-permute-start(f32[1,14,128,128]{3,2,1,0:T(8,128)S(1)} %get-tuple-element.237), channel_id=1, source_target_pairs={{0,16},{8,24},{16,0},{24,8},{1,17},{9,25},{17,1},{25,9},{2,18},{10... | collective-permute-start | bytes 2752520 | tf_op jit(solution)/shard_map/cond/branch_3_fun/ppermute | solution.py:440
  30.9 20.2 %collective-permute-done.28.refs_2_ = f32[1,14,128,128]{3,2,1,0:T(8,128)S(1)} collective-permute-done((f32[1,14,128,128]{3,2,1,0:T(8,128)S(1)}, f32[1,14,128,128]{3,2,1,0:T(8,128)S(1)}, u32[]{:S(2)}, u32[]{:S(2)}) %collective-permute-start.28) | collective-permute-done | bytes 917536 | tf_op jit(solution)/shard_map/cond/branch_3_fun/ppermute | solution.py:440
  51.1 1.3 %collective-permute-start.29 = (f32[1,14,128,128]{3,2,1,0:T(8,128)S(1)}, f32[1,14,128,128]{3,2,1,0:T(8,128)S(1)}, u32[]{:S(2)}, u32[]{:S(2)}) collective-permute-start(f32[1,14,128,128]{3,2,1,0:T(8,128)S(1)} %collective-permute-done.28.refs_2_), channel_id=1, source_target_pairs={{0,8},{8,0},{16,24},{24,16},{1,9},{9,1},{17,25},{25,17},{2,10},{10... | collective-permute-start | bytes 2752520 | tf_op jit(solution)/shard_map/cond/branch_3_fun/ppermute | solution.py:448
  52.3 1.3 %collective-permute-start.24 = (f32[1,8,128,128]{3,2,1,0:T(8,128)S(1)}, f32[1,8,128,128]{3,2,1,0:T(8,128)S(1)}, u32[]{:S(2)}, u32[]{:S(2)}) collective-permute-start(f32[1,8,128,128]{3,2,1,0:T(8,128)S(1)} %get-tuple-element.234), channel_id=1, source_target_pairs={{0,16},{8,24},{16,0},{24,8},{1,17},{9,25},{17,1},{25,9},{2,18},{10... | collective-permute-start | bytes 1572872 | tf_op jit(solution)/shard_map/cond/branch_3_fun/ppermute | solution.py:440
  53.7 7.0 %list.12 = (s32[112]{0:T(128)S(1)}, s32[112]{0:T(128)S(1)}, s32[112]{0:T(128)S(1)}, s32[5]{0:T(128)S(1)}) custom-call(s32[3]{0:T(128)S(1)} %get-tuple-element.223.me, s32[32,135]{1,0:T(8,128)S(1)} %get-tuple-element.224.gs, s32[1,2,112]{2,1,0:T(2,128)S(1)} %get-tuple-element.225.pos), custom_call_target="tpu_custom_call" | custom-call | flops 5000000000 | bytes 100000 | tf_op jit(solution)/shard_map/cond/branch_3_fun/list/pallas_call | solution.py:452
  60.7 5.1 %collective-permute-done.24.refs_0_ = f32[1,8,128,128]{3,2,1,0:T(8,128)S(1)} collective-permute-done((f32[1,8,128,128]{3,2,1,0:T(8,128)S(1)}, f32[1,8,128,128]{3,2,1,0:T(8,128)S(1)}, u32[]{:S(2)}, u32[]{:S(2)}) %collective-permute-start.24) | collective-permute-done | bytes 524320 | tf_op jit(solution)/shard_map/cond/branch_3_fun/ppermute | solution.py:440
  65.8 0.9 collective-permute-start.25
  66.7 2.8 %products.49 = f32[4,128,128]{2,1,0:T(8,128)S(1)} custom-call(s32[3]{0:T(128)S(1)} %get-tuple-element.223.me, s32[112]{0:T(128)S(1)} %get-tuple-element.226.src, s32[112]{0:T(128)S(1)} %get-tuple-element.227.aidx, s32[112]{0:T(128)S(1)} %get-tuple-element.228.oidx, s32[5]{0:T(128)S(1)} %get-tuple-element.229.starts, f32[112,128,128]{2,1,0:T(8,128)S(1)} %bitcast.60, ...), custom_call_target="tpu_custom_call" | custom-call | flops 5000000000 | bytes 1000000 | tf_op jit(solution)/shard_map/cond/branch_3_fun/products/pallas_call | solution.py:472
  69.5 1.2 %collective-permute-start.30 = (f32[4,128,128]{2,1,0:T(8,128)S(1)}, f32[4,128,128]{2,1,0:T(8,128)S(1)}, u32[]{:S(2)}, u32[]{:S(2)}) collective-permute-start(f32[4,128,128]{2,1,0:T(8,128)S(1)} %products.49), channel_id=1, source_target_pairs={{0,1},{1,0},{2,3},{3,2},{4,5},{5,4},{6,7},{7,6},{8,9},{9,8},{10,11... | collective-permute-start | bytes 786440 | tf_op jit(solution)/shard_map/cond/branch_3_fun/ppermute | solution.py:496
  70.7 15.3 %collective-permute-done.26.refs_6_.refs_4_ = f32[7,128,128]{2,1,0:T(8,128)S(1)} collective-permute-done((f32[7,128,128]{2,1,0:T(8,128)S(1)}, f32[7,128,128]{2,1,0:T(8,128)S(1)}, u32[]{:S(2)}, u32[]{:S(2)}) %collective-permute-start.26) | collective-permute-done | bytes 458784 | tf_op jit(solution)/shard_map/cond/branch_3_fun/ppermute | solution.py:369
  86.0 4.1 %products.50 = f32[4,128,128]{2,1,0:T(8,128)S(1)} custom-call(s32[3]{0:T(128)S(1)} %get-tuple-element.223.me, s32[112]{0:T(128)S(1)} %get-tuple-element.226.src, s32[112]{0:T(128)S(1)} %get-tuple-element.227.aidx, s32[112]{0:T(128)S(1)} %get-tuple-element.228.oidx, s32[5]{0:T(128)S(1)} %get-tuple-element.229.starts, f32[112,128,128]{2,1,0:T(8,128)S(1)} %bitcast.60, ...), custom_call_target="tpu_custom_call" | custom-call | flops 5000000000 | bytes 1000000 | tf_op jit(solution)/shard_map/cond/branch_3_fun/products/pallas_call | solution.py:472
  90.1 4.6 %products.48.refs_6_ = f32[8,128,128]{2,1,0:T(8,128)S(1)} custom-call(s32[3]{0:T(128)S(1)} %get-tuple-element.223.me, s32[112]{0:T(128)S(1)} %get-tuple-element.226.src, s32[112]{0:T(128)S(1)} %get-tuple-element.227.aidx, s32[112]{0:T(128)S(1)} %get-tuple-element.228.oidx, s32[5]{0:T(128)S(1)} %get-tuple-element.229.starts, f32[112,128,128]{2,1,0:T(8,128)S(1)} %bitcast.60, ...), custom_call_target="tpu_custom_call" | custom-call | flops 5000000000 | bytes 1000000 | tf_op jit(solution)/shard_map/cond/branch_3_fun/products/pallas_call | solution.py:472
  94.8 2.2 %collective-permute-done.31.refs_8_ = f32[4,128,128]{2,1,0:T(8,128)S(1)} collective-permute-done((f32[4,128,128]{2,1,0:T(8,128)S(1)}, f32[4,128,128]{2,1,0:T(8,128)S(1)}, u32[]{:S(2)}, u32[]{:S(2)}) %collective-permute-start.31) | collective-permute-done | bytes 262176 | tf_op jit(solution)/shard_map/cond/branch_3_fun/ppermute | solution.py:496
  97.0 2.8 %products.51 = f32[8,128,128]{2,1,0:T(8,128)S(1)} custom-call(s32[3]{0:T(128)S(1)} %get-tuple-element.223.me, s32[112]{0:T(128)S(1)} %get-tuple-element.226.src, s32[112]{0:T(128)S(1)} %get-tuple-element.227.aidx, s32[112]{0:T(128)S(1)} %get-tuple-element.228.oidx, s32[5]{0:T(128)S(1)} %get-tuple-element.229.starts, ...), custom_call_target="tpu_custom_call" | custom-call | flops 5000000000 | bytes 1000000 | tf_op jit(solution)/shard_map/cond/branch_3_fun/products/pallas_call | solution.py:472
  100.3 0.8 copy-done.12
  (28 shorter events, 2.9 us)
Async XLA Ops:
  0.0 27.3 %collective-permute-start.70 = (f32[112,128,128]{2,1,0:T(8,128)}, f32[112,128,128]{2,1,0:T(8,128)}, u32[]{:S(2)}, u32[]{:S(2)}) collective-permute-start(f32[112,128,128]{2,1,0:T(8,128)} %bitcast.43), channel_id=1, source_target_pairs={{0,8},{8,0},{16,24},{24,16},{1,9},{9,1},{17,25},{25,17},{2,10},{10... | collective-permute-start | bytes 22020104 | tf_op jit(solution)/shard_map/ppermute | solution.py:391
  0.7 0.7 copy-start
  1.4 0.7 copy-start.1
  2.0 0.7 copy-start.2
  9.6 17.6 %collective-permute-start.71 = (f32[7,128,128]{2,1,0:T(8,128)}, f32[7,128,128]{2,1,0:T(8,128)S(1)}, u32[]{:S(2)}, u32[]{:S(2)}) collective-permute-start(f32[7,128,128]{2,1,0:T(8,128)} %bitcast.71), channel_id=1, source_target_pairs={{0,2},{2,4},{4,6},{6,0},{1,3},{3,5},{5,7},{7,1},{8,10},{10,12},{12... | collective-permute-start | bytes 1376264 | tf_op jit(solution)/shard_map/ppermute | solution.py:369
  13.7 9.4 %all-to-all-start = ((s32[8,4,135]{2,1,0:T(4,128)}), s32[8,4,135]{2,1,0:T(4,128)S(1)}, u32[]{:S(2)}, u32[]{:S(2)}) async-start(s32[8,4,135]{2,1,0:T(4,128)} %broadcast_in_dim.2), calls=%async_computation | async-start | bytes 65536 | tf_op jit(solution)/shard_map/all_to_all | solution.py:394
  27.3 26.3 %copy-start.6 = (f32[7,128,128]{2,1,0:T(8,128)S(1)}, f32[7,128,128]{2,1,0:T(8,128)}, u32[]{:S(2)}) copy-start(f32[7,128,128]{2,1,0:T(8,128)} %get-tuple-element.235.refs_4_.refs_2_) | copy-start | bytes 1376260 | tf_op jit(solution)/shard_map/cond
  27.3 39.3 %slice-start.6 = ((s8[7340032]{0:T(1024)(128)(4,1)}), s8[4194304]{0:T(1024)(128)(4,1)S(1)}, s32[]{:S(2)}) async-start(s8[7340032]{0:T(1024)(128)(4,1)} %bitcast.59), calls=%async_computation.7 | async-start | bytes 8388608 | tf_op jit(solution)/shard_map/cond
  29.5 21.6 %collective-permute-start.28 = (f32[1,14,128,128]{3,2,1,0:T(8,128)S(1)}, f32[1,14,128,128]{3,2,1,0:T(8,128)S(1)}, u32[]{:S(2)}, u32[]{:S(2)}) collective-permute-start(f32[1,14,128,128]{3,2,1,0:T(8,128)S(1)} %get-tuple-element.237), channel_id=1, source_target_pairs={{0,16},{8,24},{16,0},{24,8},{1,17},{9,25},{17,1},{25,9},{2,18},{10... | collective-permute-start | bytes 2752520 | tf_op jit(solution)/shard_map/cond/branch_3_fun/ppermute | solution.py:440
  51.1 15.6 %collective-permute-start.29 = (f32[1,14,128,128]{3,2,1,0:T(8,128)S(1)}, f32[1,14,128,128]{3,2,1,0:T(8,128)S(1)}, u32[]{:S(2)}, u32[]{:S(2)}) collective-permute-start(f32[1,14,128,128]{3,2,1,0:T(8,128)S(1)} %collective-permute-done.28.refs_2_), channel_id=1, source_target_pairs={{0,8},{8,0},{16,24},{24,16},{1,9},{9,1},{17,25},{25,17},{2,10},{10... | collective-permute-start | bytes 2752520 | tf_op jit(solution)/shard_map/cond/branch_3_fun/ppermute | solution.py:448
  52.3 13.5 %collective-permute-start.24 = (f32[1,8,128,128]{3,2,1,0:T(8,128)S(1)}, f32[1,8,128,128]{3,2,1,0:T(8,128)S(1)}, u32[]{:S(2)}, u32[]{:S(2)}) collective-permute-start(f32[1,8,128,128]{3,2,1,0:T(8,128)S(1)} %get-tuple-element.234), channel_id=1, source_target_pairs={{0,16},{8,24},{16,0},{24,8},{1,17},{9,25},{17,1},{25,9},{2,18},{10... | collective-permute-start | bytes 1572872 | tf_op jit(solution)/shard_map/cond/branch_3_fun/ppermute | solution.py:440
  53.6 17.0 %collective-permute-start.27 = (f32[7,128,128]{2,1,0:T(8,128)S(1)}, f32[7,128,128]{2,1,0:T(8,128)S(1)}, u32[]{:S(2)}, u32[]{:S(2)}) collective-permute-start(f32[7,128,128]{2,1,0:T(8,128)S(1)} %copy-done.6), channel_id=1, source_target_pairs={{0,6},{2,0},{4,2},{6,4},{1,7},{3,1},{5,3},{7,5},{8,14},{10,8},{12,... | collective-permute-start | bytes 1376264 | tf_op jit(solution)/shard_map/cond/branch_3_fun/ppermute | solution.py:369
  53.6 32.4 %collective-permute-start.26 = (f32[7,128,128]{2,1,0:T(8,128)S(1)}, f32[7,128,128]{2,1,0:T(8,128)S(1)}, u32[]{:S(2)}, u32[]{:S(2)}) collective-permute-start(f32[7,128,128]{2,1,0:T(8,128)S(1)} %copy-done.6), channel_id=1, source_target_pairs={{0,4},{2,6},{4,0},{6,2},{1,5},{3,7},{5,1},{7,3},{8,12},{10,14},{12... | collective-permute-start | bytes 1376264 | tf_op jit(solution)/shard_map/cond/branch_3_fun/ppermute | solution.py:369
  53.6 13.0 %slice-start.7 = ((s8[7340032]{0:T(1024)(128)(4,1)}), s8[3145728]{0:T(1024)(128)(4,1)S(1)}, s32[]{:S(2)}) async-start(s8[7340032]{0:T(1024)(128)(4,1)} %bitcast.59), calls=%async_computation.8 | async-start | bytes 6291456 | tf_op jit(solution)/shard_map/cond
  65.8 29.0 %collective-permute-start.25 = (f32[1,8,128,128]{3,2,1,0:T(8,128)S(1)}, f32[1,8,128,128]{3,2,1,0:T(8,128)S(1)}, u32[]{:S(2)}, u32[]{:S(2)}) collective-permute-start(f32[1,8,128,128]{3,2,1,0:T(8,128)S(1)} %collective-permute-done.24.refs_0_), channel_id=1, source_target_pairs={{0,8},{8,0},{16,24},{24,16},{1,9},{9,1},{17,25},{25,17},{2,10},{10... | collective-permute-start | bytes 1572872 | tf_op jit(solution)/shard_map/cond/branch_3_fun/ppermute | solution.py:448
  69.5 25.3 %collective-permute-start.30 = (f32[4,128,128]{2,1,0:T(8,128)S(1)}, f32[4,128,128]{2,1,0:T(8,128)S(1)}, u32[]{:S(2)}, u32[]{:S(2)}) collective-permute-start(f32[4,128,128]{2,1,0:T(8,128)S(1)} %products.49), channel_id=1, source_target_pairs={{0,1},{1,0},{2,3},{3,2},{4,5},{5,4},{6,7},{7,6},{8,9},{9,8},{10,11... | collective-permute-start | bytes 786440 | tf_op jit(solution)/shard_map/cond/branch_3_fun/ppermute | solution.py:496
  90.1 7.0 %collective-permute-start.31 = (f32[4,128,128]{2,1,0:T(8,128)S(1)}, f32[4,128,128]{2,1,0:T(8,128)S(1)}, u32[]{:S(2)}, u32[]{:S(2)}) collective-permute-start(f32[4,128,128]{2,1,0:T(8,128)S(1)} %products.50), channel_id=1, source_target_pairs={{0,1},{1,0},{2,3},{3,2},{4,5},{5,4},{6,7},{7,6},{8,9},{9,8},{10,11... | collective-permute-start | bytes 786440 | tf_op jit(solution)/shard_map/cond/branch_3_fun/ppermute | solution.py:496
  100.3 0.8 copy-start.12
where the time goes:
time: 101 us
  waiting for transfers between devices  46.1 us (46%)
  Pallas kernels  28.1 us (28%)
  starting transfers between devices  16.4 us (16%)
  blocking collectives  5.6 us (6%)
  local copies, waits for them, and re-layouts  3.49 us (3%)
    ppermute x2, waiting for transfers between devices, across(): lax.ppermute(packed[k - 1:k], 'row', [(r, (r // PAIR + k) % Y * PAIR + r...  25.3 us
    ppermute x3, waiting for transfers between devices, shift(): return lax.ppermute(x, 'col', [(c, (c + k) % G) for c in range(G)])  15.3 us
    pallas_call x4, Pallas kernels, products(): pl.pallas_call(functools.partial(product_kernel, d, k, depth, first, len(...  14.2 us
    pallas_call x1, Pallas kernels, body(): pl.pallas_call(functools.partial(list_kernel, d, first), in_specs=[smem,...  7.03 us
    all_to_all x1, starting transfers between devices, on_device(): lax.all_to_all(jnp.broadcast_to(group[None], (R * L, G, n_idx)), ('row',...  6.13 us
    all_gather x1, blocking collectives, on_device(): group = lax.all_gather(idx, 'col', axis=0, tiled=True)  5.6 us
    ppermute x3, starting transfers between devices, shift(): return lax.ppermute(x, 'col', [(c, (c + k) % G) for c in range(G)])  3.5 us
    pallas_call x1, Pallas kernels, on_device(): pl.pallas_call(functools.partial(plan_kernel, d), in_specs=[smem, smem, v...  3.38 us
  transfers between devices with their start and end apart: 11, of which 5 were waited for; matrix products, arithmetic and copies ran while one was open for 1% of the time, Pallas kernels for 23%

commit v1 on v0

--- a/solution.py
+++ b/solution.py
@@ -10,6 +10,7 @@
 
 
 AXES = ("row", "col", "layer")
+LADDER = ((10, 18), (11, 20), (12, 22), (13, 24), (14, 26), (16, 28), (20, 36), (36, 64), (112, 112))
 SMEM = pltpu.SMEM
 VMEM = pltpu.VMEM
 HBM = pltpu.HBM
@@ -18,7 +19,13 @@
 BF16 = jnp.bfloat16
 
 
-def index_kernel(d, b_rows, a_cols, c_cols, out):
+def index_kernel(d, b_in, a_in, c_in, out, b_rows, a_cols, c_cols, sem):
+    pairs = ((b_in, b_rows), (a_in, a_cols), (c_in, c_cols))
+    copies = [pltpu.make_async_copy(x, y, sem.at[k]) for k, (x, y) in enumerate(pairs)]
+    for copy in copies:
+        copy.start()
+    for copy in copies:
+        copy.wait()
     for w in range(d.W):
         for s in range(d.S):
             out[0, w * d.S + s] = b_rows[s, 0, w]
@@ -352,8 +359,8 @@
     d.Y, d.NB, d.N, d.QL = d.R // d.PAIR, d.W * d.S, d.R * d.G * d.L, d.Q // d.L
     d.OFF_C = d.NB + d.AR * d.SA
     d.EARLY = 1 + max(1, d.G // 4)
-    totals = sorted({-(-d.NB * k // 56) for k in (8, 9, 10, 11, 12, 14, 18, 28)})
-    d.caps = tuple((-(-t * 5 // 8), t) for t in totals) + ((d.NB, d.NB),)
+    ladder = {(-(-d.NB * f // 112), -(-d.NB * t // 112)) for f, t in LADDER}
+    d.caps = tuple(sorted(ladder))
     d.sections = tuple(
         (step, low, high, None)
         for step in range(1, d.L)
@@ -381,19 +388,24 @@
 
     idx = pl.pallas_call(
         functools.partial(index_kernel, d),
-        in_specs=[smem] * 3,
+        in_specs=[hbm] * 3,
         out_specs=smem,
         out_shape=jax.ShapeDtypeStruct((1, n_idx), I32),
-        compiler_params=limit(),
+        scratch_shapes=[
+            SMEM((d.S, 1, d.W), I32),
+            SMEM(a_cols.shape, I32),
+            SMEM(c_cols.shape, I32),
+            pltpu.SemaphoreType.DMA((3,)),
+        ],
+        compiler_params=pltpu.CompilerParams(vmem_limit_bytes=60 << 20),
         name="index",
     )(b_rows.transpose(2, 1, 0), a_cols, c_cols)
     group = lax.all_gather(idx, "col", axis=0, tiled=True)
     sib = lax.ppermute(own, "row", pair_swap)
-    a_from, group = lax.optimization_barrier((a_own, group))
+    spread = jnp.broadcast_to(group[None], (R * L, G, n_idx))
+    a_from, spread = lax.optimization_barrier((a_own, spread))
     a_early = [a_own] + [shift(a_from, k) for k in range(1, d.EARLY)]
-    table = lax.all_to_all(
-        jnp.broadcast_to(group[None], (R * L, G, n_idx)), ("row", "layer"), 0, 0, tiled=True
-    )
+    table = lax.all_to_all(spread, ("row", "layer"), 0, 0, tiled=True)
     table = table.reshape(R, L, G, n_idx).transpose(0, 2, 1, 3).reshape(d.N, n_idx)
 
     inv, cnt, pos, level = pl.pallas_call(

time: 101 us -> 99.7 us (0.987)
  local copies, waits for them, and re-layouts: 3.49 us -> 1.48 us
    ppermute x3, waiting for transfers between devices: 15.3 us -> 9.72 us  [shift(): return lax.ppermute(x, 'col', [(c, (c + k) % G) for c in range(G)])]
    ppermute x2, waiting for transfers between devices: 25.3 us -> 30.9 us  [across(): lax.ppermute(packed[k - 1:k], 'row', [(r, (r // PAIR + k) % Y * PAIR + r...]
    unnamed x9 -> x3, local copies, waits for them, and re-layouts: 2.81 us -> 0.79 us
where the time goes in v1:
time: 99.7 us; the launch traced here: 99.4 us
  waiting for transfers between devices  46.1 us (46%)
  Pallas kernels  28.2 us (28%)
  starting transfers between devices  16.4 us (16%)
  blocking collectives  5.84 us (6%)
  local copies, waits for them, and re-layouts  1.48 us (1%)
    ppermute x2, waiting for transfers between devices, across(): lax.ppermute(packed[k - 1:k], 'row', [(r, (r // PAIR + k) % Y * PAIR + r...  30.9 us
    pallas_call x4, Pallas kernels, products(): pl.pallas_call(functools.partial(product_kernel, d, k, depth, first, len(...  14.2 us
    ppermute x3, waiting for transfers between devices, shift(): return lax.ppermute(x, 'col', [(c, (c + k) % G) for c in range(G)])  9.72 us
    pallas_call x1, Pallas kernels, body(): pl.pallas_call(functools.partial(list_kernel, d, first), in_specs=[smem,...  7.03 us
    all_to_all x1, starting transfers between devices, on_device(): table = lax.all_to_all(spread, ('row', 'layer'), 0, 0, tiled=True)  6.13 us
    all_gather x1, blocking collectives, on_device(): group = lax.all_gather(idx, 'col', axis=0, tiled=True)  5.84 us
    ppermute x3, starting transfers between devices, shift(): return lax.ppermute(x, 'col', [(c, (c + k) % G) for c in range(G)])  3.5 us
    pallas_call x1, Pallas kernels, on_device(): pl.pallas_call(functools.partial(plan_kernel, d), in_specs=[smem, smem, v...  3.38 us
  transfers between devices with their start and end apart: 11, of which 5 were waited for; matrix products, arithmetic and copies ran while one was open for 1% of the time, Pallas kernels for 23%

profile of v1, /device:TPU:29, one launch (start us, length us, event | category | flops | bytes accessed | tf_op | source)
XLA Modules:
  0.0 99.4 jit_solution(3887965022286249360)
XLA Ops:
  0.0 0.7 collective-permute-start.70
  0.7 1.4 %index.1 = s32[1,135]{1,0:T(1,128)} custom-call(s32[7,1,16]{2,1,0:T(1,128)} %bitcast.82, s32[1,1,7]{2,1,0:T(1,128)} %a_in.1, s32[4,1,4]{2,1,0:T(1,128)} %c_in.1), custom_call_target="tpu_custom_call" | custom-call | tf_op jit(solution)/shard_map/index/pallas_call | solution.py:389
  2.1 5.8 %all-gather = s32[4,1,135]{2,1,0:T(1,128)S(1)} all-gather(s32[1,1,135]{2,1,0:T(1,128)} %bitcast.81), channel_id=1, replica_groups=mesh['row'=4,'col'=4,'layer'=2] {'col'}, dimensions={0}, use_global_device_ids=true | all-gather | bytes 2700 | tf_op jit(solution)/shard_map/all_gather | solution.py:403
  8.6 3.5 %collective-permute-start.71 = (f32[7,128,128]{2,1,0:T(8,128)}, f32[7,128,128]{2,1,0:T(8,128)S(1)}, u32[]{:S(2)}, u32[]{:S(2)}) collective-permute-start(f32[7,128,128]{2,1,0:T(8,128)} %bitcast.69), channel_id=1, source_target_pairs={{0,2},{2,4},{4,6},{6,0},{1,3},{3,5},{5,7},{7,1},{8,10},{10,12},{12... | collective-permute-start | bytes 1376264 | tf_op jit(solution)/shard_map/ppermute | solution.py:376
  12.1 6.1 %all-to-all-start = ((s32[8,4,135]{2,1,0:T(4,128)}), s32[8,4,135]{2,1,0:T(4,128)S(1)}, u32[]{:S(2)}, u32[]{:S(2)}) async-start(s32[8,4,135]{2,1,0:T(4,128)} %broadcast_in_dim.2), calls=%async_computation | async-start | bytes 65536 | tf_op jit(solution)/shard_map/all_to_all | solution.py:408
  18.3 3.2 %all-to-all-done = s32[8,4,135]{2,1,0:T(4,128)S(1)} async-done(((s32[8,4,135]{2,1,0:T(4,128)}), s32[8,4,135]{2,1,0:T(4,128)S(1)}, u32[]{:S(2)}, u32[]{:S(2)}) %all-to-all-start) | async-done | bytes 17312 | tf_op jit(solution)/shard_map/all_to_all | solution.py:408
  21.6 3.4 %plan.1 = (s32[1,2,224]{2,1,0:T(2,128)S(1)}, s32[1,2]{1,0:T(1,128)S(1)}, s32[1,2,112]{2,1,0:T(2,128)S(1)}, s32[1]{0:T(128)}) custom-call(s32[3]{0:T(128)S(1)} %pad_add_fusion.me, s32[32,135]{1,0:T(8,128)S(1)} %reshape.46.gs.gv, s32[32,135]{1,0:T(8,128)S(1)} %reshape.46.gs.gv), custom_call_target="tpu_custom_call" | custom-call | tf_op jit(solution)/shard_map/plan/pallas_call | solution.py:411
  25.6 73.0 %conditional.1 = (f32[4,1,2,128,128]{4,3,2,1,0:T(8,128)S(1)}) conditional(s32[]{:T(128)} %bitcast.35, (s32[3]{0:T(128)S(1)}, s32[32,135]{1,0:T(8,128)S(1)}, s32[1,2,112]{2,1,0:T(2,128)S(1)}, s32[1,2,224]{2,1,0:T(2,128)S(1)}, s32[1,2]{1,0:T(1,128)S(1)}, /*index=5*/f32[112,128,128]{2,1,0:T(8,128)}, ...), branch_computations={%region_0.0_spmd, %region_1.0_spmd, %region_2.0_spmd, %region_3.0_... | conditional | flops 24999999488 | bytes 92442856 | solution.py:512
  25.8 2.1 %pack.13 = (f32[1,14,128,128]{3,2,1,0:T(8,128)S(1)}, f32[1,12,128,128]{3,2,1,0:T(8,128)S(1)}) custom-call(s32[3]{0:T(128)S(1)} %get-tuple-element.238.me, s32[1,2,224]{2,1,0:T(2,128)S(1)} %get-tuple-element.245.inv, s32[1,2]{1,0:T(1,128)S(1)} %get-tuple-element.246.cnt, f32[112,128,128]{2,1,0:T(8,128)} %get-tuple-element.247.own.refs_0_, ...), custom_call_target="tpu_custom_call" | custom-call | tf_op jit(solution)/shard_map/cond/branch_4_fun/pack/pallas_call | solution.py:436
  28.0 1.4 %collective-permute-start.36 = (f32[1,14,128,128]{3,2,1,0:T(8,128)S(1)}, f32[1,14,128,128]{3,2,1,0:T(8,128)S(1)}, u32[]{:S(2)}, u32[]{:S(2)}) collective-permute-start(f32[1,14,128,128]{3,2,1,0:T(8,128)S(1)} %get-tuple-element.252), channel_id=1, source_target_pairs={{0,16},{8,24},{16,0},{24,8},{1,17},{9,25},{17,1},{25,9},{2,18},{10... | collective-permute-start | bytes 2752520 | tf_op jit(solution)/shard_map/cond/branch_4_fun/ppermute | solution.py:452
  29.4 20.2 %collective-permute-done.36.refs_2_ = f32[1,14,128,128]{3,2,1,0:T(8,128)S(1)} collective-permute-done((f32[1,14,128,128]{3,2,1,0:T(8,128)S(1)}, f32[1,14,128,128]{3,2,1,0:T(8,128)S(1)}, u32[]{:S(2)}, u32[]{:S(2)}) %collective-permute-start.36) | collective-permute-done | bytes 917536 | tf_op jit(solution)/shard_map/cond/branch_4_fun/ppermute | solution.py:452
  49.6 1.3 %collective-permute-start.37 = (f32[1,14,128,128]{3,2,1,0:T(8,128)S(1)}, f32[1,14,128,128]{3,2,1,0:T(8,128)S(1)}, u32[]{:S(2)}, u32[]{:S(2)}) collective-permute-start(f32[1,14,128,128]{3,2,1,0:T(8,128)S(1)} %collective-permute-done.36.refs_2_), channel_id=1, source_target_pairs={{0,8},{8,0},{16,24},{24,16},{1,9},{9,1},{17,25},{25,17},{2,10},{10... | collective-permute-start | bytes 2752520 | tf_op jit(solution)/shard_map/cond/branch_4_fun/ppermute | solution.py:460
  50.8 1.3 %collective-permute-start.32 = (f32[1,12,128,128]{3,2,1,0:T(8,128)S(1)}, f32[1,12,128,128]{3,2,1,0:T(8,128)S(1)}, u32[]{:S(2)}, u32[]{:S(2)}) collective-permute-start(f32[1,12,128,128]{3,2,1,0:T(8,128)S(1)} %get-tuple-element.249), channel_id=1, source_target_pairs={{0,16},{8,24},{16,0},{24,8},{1,17},{9,25},{17,1},{25,9},{2,18},{10... | collective-permute-start | bytes 2359304 | tf_op jit(solution)/shard_map/cond/branch_4_fun/ppermute | solution.py:452
  52.2 7.0 %list.13 = (s32[112]{0:T(128)S(1)}, s32[112]{0:T(128)S(1)}, s32[112]{0:T(128)S(1)}, s32[5]{0:T(128)S(1)}) custom-call(s32[3]{0:T(128)S(1)} %get-tuple-element.238.me, s32[32,135]{1,0:T(8,128)S(1)} %get-tuple-element.239.gs, s32[1,2,112]{2,1,0:T(2,128)S(1)} %get-tuple-element.240.pos), custom_call_target="tpu_custom_call" | custom-call | flops 5000000000 | bytes 100000 | tf_op jit(solution)/shard_map/cond/branch_4_fun/list/pallas_call | solution.py:464
  59.2 10.7 %collective-permute-done.32.refs_0_ = f32[1,12,128,128]{3,2,1,0:T(8,128)S(1)} collective-permute-done((f32[1,12,128,128]{3,2,1,0:T(8,128)S(1)}, f32[1,12,128,128]{3,2,1,0:T(8,128)S(1)}, u32[]{:S(2)}, u32[]{:S(2)}) %collective-permute-start.32) | collective-permute-done | bytes 786464 | tf_op jit(solution)/shard_map/cond/branch_4_fun/ppermute | solution.py:452
  69.9 0.9 collective-permute-start.33
  70.8 2.8 %products.53 = f32[4,128,128]{2,1,0:T(8,128)S(1)} custom-call(s32[3]{0:T(128)S(1)} %get-tuple-element.238.me, s32[112]{0:T(128)S(1)} %get-tuple-element.241.src, s32[112]{0:T(128)S(1)} %get-tuple-element.242.aidx, s32[112]{0:T(128)S(1)} %get-tuple-element.243.oidx, s32[5]{0:T(128)S(1)} %get-tuple-element.244.starts, f32[112,128,128]{2,1,0:T(8,128)S(1)} %bitcast.60, ...), custom_call_target="tpu_custom_call" | custom-call | flops 5000000000 | bytes 1000000 | tf_op jit(solution)/shard_map/cond/branch_4_fun/products/pallas_call | solution.py:484
  73.6 1.2 %collective-permute-start.38 = (f32[4,128,128]{2,1,0:T(8,128)S(1)}, f32[4,128,128]{2,1,0:T(8,128)S(1)}, u32[]{:S(2)}, u32[]{:S(2)}) collective-permute-start(f32[4,128,128]{2,1,0:T(8,128)S(1)} %products.53), channel_id=1, source_target_pairs={{0,1},{1,0},{2,3},{3,2},{4,5},{5,4},{6,7},{7,6},{8,9},{9,8},{10,11... | collective-permute-start | bytes 786440 | tf_op jit(solution)/shard_map/cond/branch_4_fun/ppermute | solution.py:508
  74.8 9.7 %collective-permute-done.34.refs_6_.refs_4_ = f32[7,128,128]{2,1,0:T(8,128)S(1)} collective-permute-done((f32[7,128,128]{2,1,0:T(8,128)S(1)}, f32[7,128,128]{2,1,0:T(8,128)S(1)}, u32[]{:S(2)}, u32[]{:S(2)}) %collective-permute-start.34) | collective-permute-done | bytes 458784 | tf_op jit(solution)/shard_map/cond/branch_4_fun/ppermute | solution.py:376
  84.5 4.1 %products.54 = f32[4,128,128]{2,1,0:T(8,128)S(1)} custom-call(s32[3]{0:T(128)S(1)} %get-tuple-element.238.me, s32[112]{0:T(128)S(1)} %get-tuple-element.241.src, s32[112]{0:T(128)S(1)} %get-tuple-element.242.aidx, s32[112]{0:T(128)S(1)} %get-tuple-element.243.oidx, s32[5]{0:T(128)S(1)} %get-tuple-element.244.starts, f32[112,128,128]{2,1,0:T(8,128)S(1)} %bitcast.60, ...), custom_call_target="tpu_custom_call" | custom-call | flops 5000000000 | bytes 1000000 | tf_op jit(solution)/shard_map/cond/branch_4_fun/products/pallas_call | solution.py:484
  88.6 4.6 %products.52.refs_6_ = f32[8,128,128]{2,1,0:T(8,128)S(1)} custom-call(s32[3]{0:T(128)S(1)} %get-tuple-element.238.me, s32[112]{0:T(128)S(1)} %get-tuple-element.241.src, s32[112]{0:T(128)S(1)} %get-tuple-element.242.aidx, s32[112]{0:T(128)S(1)} %get-tuple-element.243.oidx, s32[5]{0:T(128)S(1)} %get-tuple-element.244.starts, f32[112,128,128]{2,1,0:T(8,128)S(1)} %bitcast.60, ...), custom_call_target="tpu_custom_call" | custom-call | flops 5000000000 | bytes 1000000 | tf_op jit(solution)/shard_map/cond/branch_4_fun/products/pallas_call | solution.py:484
  93.3 2.2 %collective-permute-done.39.refs_8_ = f32[4,128,128]{2,1,0:T(8,128)S(1)} collective-permute-done((f32[4,128,128]{2,1,0:T(8,128)S(1)}, f32[4,128,128]{2,1,0:T(8,128)S(1)}, u32[]{:S(2)}, u32[]{:S(2)}) %collective-permute-start.39) | collective-permute-done | bytes 262176 | tf_op jit(solution)/shard_map/cond/branch_4_fun/ppermute | solution.py:508
  95.5 2.8 %products.55 = f32[8,128,128]{2,1,0:T(8,128)S(1)} custom-call(s32[3]{0:T(128)S(1)} %get-tuple-element.238.me, s32[112]{0:T(128)S(1)} %get-tuple-element.241.src, s32[112]{0:T(128)S(1)} %get-tuple-element.242.aidx, s32[112]{0:T(128)S(1)} %get-tuple-element.243.oidx, s32[5]{0:T(128)S(1)} %get-tuple-element.244.starts, ...), custom_call_target="tpu_custom_call" | custom-call | flops 5000000000 | bytes 1000000 | tf_op jit(solution)/shard_map/cond/branch_4_fun/products/pallas_call | solution.py:484
  98.6 0.8 copy-done.9
  (22 shorter events, 0.9 us)
Async XLA Ops:
  0.0 25.6 %collective-permute-start.70 = (f32[112,128,128]{2,1,0:T(8,128)}, f32[112,128,128]{2,1,0:T(8,128)}, u32[]{:S(2)}, u32[]{:S(2)}) collective-permute-start(f32[112,128,128]{2,1,0:T(8,128)} %bitcast.41), channel_id=1, source_target_pairs={{0,8},{8,0},{16,24},{24,16},{1,9},{9,1},{17,25},{25,17},{2,10},{10... | collective-permute-start | bytes 22020104 | tf_op jit(solution)/shard_map/ppermute | solution.py:404
  8.6 17.0 %collective-permute-start.71 = (f32[7,128,128]{2,1,0:T(8,128)}, f32[7,128,128]{2,1,0:T(8,128)S(1)}, u32[]{:S(2)}, u32[]{:S(2)}) collective-permute-start(f32[7,128,128]{2,1,0:T(8,128)} %bitcast.69), channel_id=1, source_target_pairs={{0,2},{2,4},{4,6},{6,0},{1,3},{3,5},{5,7},{7,1},{8,10},{10,12},{12... | collective-permute-start | bytes 1376264 | tf_op jit(solution)/shard_map/ppermute | solution.py:376
  12.1 9.4 %all-to-all-start = ((s32[8,4,135]{2,1,0:T(4,128)}), s32[8,4,135]{2,1,0:T(4,128)S(1)}, u32[]{:S(2)}, u32[]{:S(2)}) async-start(s32[8,4,135]{2,1,0:T(4,128)} %broadcast_in_dim.2), calls=%async_computation | async-start | bytes 65536 | tf_op jit(solution)/shard_map/all_to_all | solution.py:408
  25.8 26.3 %copy-start.4 = (f32[7,128,128]{2,1,0:T(8,128)S(1)}, f32[7,128,128]{2,1,0:T(8,128)}, u32[]{:S(2)}) copy-start(f32[7,128,128]{2,1,0:T(8,128)} %get-tuple-element.250.refs_4_.refs_2_) | copy-start | bytes 1376260 | tf_op jit(solution)/shard_map/cond
  25.8 45.0 %slice-start.8 = ((s8[7340032]{0:T(1024)(128)(4,1)}), s8[4194304]{0:T(1024)(128)(4,1)S(1)}, s32[]{:S(2)}) async-start(s8[7340032]{0:T(1024)(128)(4,1)} %bitcast.59), calls=%async_computation.9 | async-start | bytes 8388608 | tf_op jit(solution)/shard_map/cond
  28.0 21.6 %collective-permute-start.36 = (f32[1,14,128,128]{3,2,1,0:T(8,128)S(1)}, f32[1,14,128,128]{3,2,1,0:T(8,128)S(1)}, u32[]{:S(2)}, u32[]{:S(2)}) collective-permute-start(f32[1,14,128,128]{3,2,1,0:T(8,128)S(1)} %get-tuple-element.252), channel_id=1, source_target_pairs={{0,16},{8,24},{16,0},{24,8},{1,17},{9,25},{17,1},{25,9},{2,18},{10... | collective-permute-start | bytes 2752520 | tf_op jit(solution)/shard_map/cond/branch_4_fun/ppermute | solution.py:452
  49.6 21.2 %collective-permute-start.37 = (f32[1,14,128,128]{3,2,1,0:T(8,128)S(1)}, f32[1,14,128,128]{3,2,1,0:T(8,128)S(1)}, u32[]{:S(2)}, u32[]{:S(2)}) collective-permute-start(f32[1,14,128,128]{3,2,1,0:T(8,128)S(1)} %collective-permute-done.36.refs_2_), channel_id=1, source_target_pairs={{0,8},{8,0},{16,24},{24,16},{1,9},{9,1},{17,25},{25,17},{2,10},{10... | collective-permute-start | bytes 2752520 | tf_op jit(solution)/shard_map/cond/branch_4_fun/ppermute | solution.py:460
  50.8 19.1 %collective-permute-start.32 = (f32[1,12,128,128]{3,2,1,0:T(8,128)S(1)}, f32[1,12,128,128]{3,2,1,0:T(8,128)S(1)}, u32[]{:S(2)}, u32[]{:S(2)}) collective-permute-start(f32[1,12,128,128]{3,2,1,0:T(8,128)S(1)} %get-tuple-element.249), channel_id=1, source_target_pairs={{0,16},{8,24},{16,0},{24,8},{1,17},{9,25},{17,1},{25,9},{2,18},{10... | collective-permute-start | bytes 2359304 | tf_op jit(solution)/shard_map/cond/branch_4_fun/ppermute | solution.py:452
  52.1 22.6 %collective-permute-start.35 = (f32[7,128,128]{2,1,0:T(8,128)S(1)}, f32[7,128,128]{2,1,0:T(8,128)S(1)}, u32[]{:S(2)}, u32[]{:S(2)}) collective-permute-start(f32[7,128,128]{2,1,0:T(8,128)S(1)} %copy-done.4), channel_id=1, source_target_pairs={{0,6},{2,0},{4,2},{6,4},{1,7},{3,1},{5,3},{7,5},{8,14},{10,8},{12,... | collective-permute-start | bytes 1376264 | tf_op jit(solution)/shard_map/cond/branch_4_fun/ppermute | solution.py:376
  52.1 32.4 %collective-permute-start.34 = (f32[7,128,128]{2,1,0:T(8,128)S(1)}, f32[7,128,128]{2,1,0:T(8,128)S(1)}, u32[]{:S(2)}, u32[]{:S(2)}) collective-permute-start(f32[7,128,128]{2,1,0:T(8,128)S(1)} %copy-done.4), channel_id=1, source_target_pairs={{0,4},{2,6},{4,0},{6,2},{1,5},{3,7},{5,1},{7,3},{8,12},{10,14},{12... | collective-permute-start | bytes 1376264 | tf_op jit(solution)/shard_map/cond/branch_4_fun/ppermute | solution.py:376
  52.2 18.6 %slice-start.9 = ((s8[7340032]{0:T(1024)(128)(4,1)}), s8[3145728]{0:T(1024)(128)(4,1)S(1)}, s32[]{:S(2)}) async-start(s8[7340032]{0:T(1024)(128)(4,1)} %bitcast.59), calls=%async_computation.10 | async-start | bytes 6291456 | tf_op jit(solution)/shard_map/cond
  69.9 23.4 %collective-permute-start.33 = (f32[1,12,128,128]{3,2,1,0:T(8,128)S(1)}, f32[1,12,128,128]{3,2,1,0:T(8,128)S(1)}, u32[]{:S(2)}, u32[]{:S(2)}) collective-permute-start(f32[1,12,128,128]{3,2,1,0:T(8,128)S(1)} %collective-permute-done.32.refs_0_), channel_id=1, source_target_pairs={{0,8},{8,0},{16,24},{24,16},{1,9},{9,1},{17,25},{25,17},{2,10},{10... | collective-permute-start | bytes 2359304 | tf_op jit(solution)/shard_map/cond/branch_4_fun/ppermute | solution.py:460
  73.6 19.7 %collective-permute-start.38 = (f32[4,128,128]{2,1,0:T(8,128)S(1)}, f32[4,128,128]{2,1,0:T(8,128)S(1)}, u32[]{:S(2)}, u32[]{:S(2)}) collective-permute-start(f32[4,128,128]{2,1,0:T(8,128)S(1)} %products.53), channel_id=1, source_target_pairs={{0,1},{1,0},{2,3},{3,2},{4,5},{5,4},{6,7},{7,6},{8,9},{9,8},{10,11... | collective-permute-start | bytes 786440 | tf_op jit(solution)/shard_map/cond/branch_4_fun/ppermute | solution.py:508
  88.6 7.0 %collective-permute-start.39 = (f32[4,128,128]{2,1,0:T(8,128)S(1)}, f32[4,128,128]{2,1,0:T(8,128)S(1)}, u32[]{:S(2)}, u32[]{:S(2)}) collective-permute-start(f32[4,128,128]{2,1,0:T(8,128)S(1)} %products.54), channel_id=1, source_target_pairs={{0,1},{1,0},{2,3},{3,2},{4,5},{5,4},{6,7},{7,6},{8,9},{9,8},{10,11... | collective-permute-start | bytes 786440 | tf_op jit(solution)/shard_map/cond/branch_4_fun/ppermute | solution.py:508
  98.6 0.8 copy-start.9

commit v2 on v1

--- a/solution.py
+++ b/solution.py
@@ -41,7 +41,13 @@
     return jnp.floor((x.astype(F32) + 0.5) * (1.0 / n)).astype(I32)
 
 
-def plan_kernel(d, me, gs, gv, inv_ref, cnt_ref, pos_ref, lvl_ref, need, need_send):
+def shift_of(d, col, slot):
+    inner = col > 0
+    shift = jnp.where(slot == 1, jnp.where(inner, 1, d.G - 1), slot)
+    return jnp.where(slot == d.G - 1, jnp.where(inner, d.G - 1, 1), shift)
+
+
+def plan_kernel(d, me, gs, gv, inv_ref, cnt_ref, pos_ref, lvl_ref, need, need_send, rows):
     b = gv[:, : d.NB]
     dev = lax.broadcasted_iota(I32, b.shape, 0)
     block = over(dev, d.L)
@@ -103,39 +109,46 @@
     y = me[0] // d.PAIR
     mine = me[1] * d.L + me[2]
     lanes = lax.broadcasted_iota(I32, (d.NB, d.PAIR * d.NB), 1).astype(F32)
-    ones = jnp.ones((8, d.NB), F32)
+    width = 2 * d.PAIR
 
     def rows_of(ref, dst, src, c):
         return ref[dst, pl.ds((src * d.PAIR + c) * d.G * d.L + mine, 1), :].astype(F32)
 
+    rows[...] = jnp.zeros(rows.shape, F32)
     for delta in range(1, d.Y):
         dst = (y + delta) % d.Y
         src = (y + d.Y - delta) % d.Y
+        for way, (to, of) in enumerate(((dst, y), (y, src))):
+            at = (2 * (delta - 1) + way) * width
+            for c in range(d.PAIR):
+                send = rows_of(need_send, to, of, c)
+                rows[at + c : at + c + 1, :] = send
+                rows[at + d.PAIR + c : at + d.PAIR + c + 1, :] = rows_of(need, to, of, c) - send
+    bits = rows[...]
+    along = jnp.dot(bits, tri, preferred_element_type=F32)
+    down = lax.dot_general(tri, bits, (((0,), (1,)), ((), ())), preferred_element_type=F32)
+    for delta in range(1, d.Y):
+        at = 2 * (delta - 1) * width
         for kind in range(2):
-            before = jnp.float32(0)
+            before = jnp.zeros((1, 1), F32)
             inv = jnp.zeros((1, d.PAIR * d.NB), F32)
             for c in range(d.PAIR):
-                bits = rows_of(need_send, dst, y, c)
-                if kind == 1:
-                    bits = rows_of(need, dst, y, c) - bits
-                wide = ones * bits
-                upto = lax.dot_general(tri, wide, (((0,), (1,)), ((), ())), preferred_element_type=F32)
+                r = at + kind * d.PAIR + c
                 inv = inv + jnp.sum(
-                    jnp.where(upto[:, :1] + before <= lanes, 1.0, 0.0), axis=0, keepdims=True
+                    jnp.where(down[:, r : r + 1] + before <= lanes, 1.0, 0.0), axis=0, keepdims=True
                 )
-                before = before + jnp.sum(bits)
+                before = before + along[r : r + 1, d.NB - 1 : d.NB]
             inv_ref[delta - 1, kind : kind + 1, :] = inv.astype(I32)
-            cnt_ref[delta - 1, kind] = before.astype(I32)
-        before = jnp.float32(0)
+            cnt_ref[delta - 1, kind] = jnp.sum(before).astype(I32)
+        at = at + width
+        before = jnp.zeros((1, 1), F32)
         position = [None] * d.PAIR
         for kind in range(2):
             for c in range(d.PAIR):
-                bits = rows_of(need_send, y, src, c)
-                if kind == 1:
-                    bits = rows_of(need, y, src, c) - bits
-                ahead = jnp.dot(ones * bits, tri, preferred_element_type=F32)[:1] - bits + before
-                position[c] = ahead if kind == 0 else jnp.where(bits > 0.5, ahead, position[c])
-                before = before + jnp.sum(bits)
+                r = at + kind * d.PAIR + c
+                ahead = along[r : r + 1] - bits[r : r + 1] + before
+                position[c] = ahead if kind == 0 else jnp.where(bits[r : r + 1] > 0.5, ahead, position[c])
+                before = before + along[r : r + 1, d.NB - 1 : d.NB]
         for c in range(d.PAIR):
             pos_ref[delta - 1, c : c + 1, :] = position[c].astype(I32)
 
@@ -197,7 +210,7 @@
             sl_d = i // (d.AR * d.QL)
             ar = i // d.QL % d.AR
             qq = i % d.QL
-            cc = (col + d.G - (low + sl_d)) % d.G
+            cc = (col + d.G - shift_of(d, col, low + sl_d)) % d.G
             ci = cc * d.AR + ar
             j = gs[(row * d.G + col) * d.L + lay, d.OFF_C + ci * d.Q + half * d.QL + qq]
             rp = j // (d.G * d.W)
@@ -234,11 +247,12 @@
     starts_ref[len(d.sections)] = n
 
 
-def product_kernel(d, section, depth, first_cap, n_a, n_x, me, src, aidx, oidx, starts, *refs):
+def product_kernel(d, section, depth, first_cap, a_fill, n_x, me, src, aidx, oidx, starts, *refs):
     last = n_x > 0
     n_local = 0 if last else 2
     local, (straight, crossed) = refs[:n_local], refs[n_local : n_local + 2]
     refs = refs[n_local + 2 :]
+    n_a = len(a_fill)
     a_refs, parts, out = refs[:n_a], refs[n_a : n_a + n_x], refs[n_a + n_x]
     a_all, buf, sem = refs[n_a + n_x + 1 :]
     core = me[0] % d.PAIR
@@ -284,16 +298,25 @@
     rows = d.AR * d.SA
     T = d.T
 
-    @pl.when(n > 0)
-    def _():
-        for k in range(n_a):
-            a = a_refs[k][...]
+    col = me[1]
+    for ref, uses in zip(a_refs, a_fill, strict=True):
+        active, slot = n < 0, jnp.int32(0)
+        for use, low, high in uses:
+            here = (col >= low) & (col < high)
+            active = active | here
+            slot = jnp.where(here, use, slot)
+
+        def split(r, _):
+            a = ref[r]
             hi = a.astype(BF16)
-            a_all[k * rows : (k + 1) * rows, :T, :] = hi
-            a_all[k * rows : (k + 1) * rows, T:, :] = (a - hi.astype(F32)).astype(BF16)
+            a_all[slot * rows + r, :T, :] = hi
+            a_all[slot * rows + r, T:, :] = (a - hi.astype(F32)).astype(BF16)
+            return 0
+
+        lax.fori_loop(0, jnp.where(active & (n > 0), rows, 0), split, 0)
 
     def place(slot):
-        return (me[1] + d.G - slot) % d.G * size
+        return (me[1] + d.G - shift_of(d, me[1], slot)) % d.G * size
 
     if last:
         for k in range(d.G):
@@ -358,7 +381,7 @@
     d.PAIR = 2 if d.R % 2 == 0 else 1
     d.Y, d.NB, d.N, d.QL = d.R // d.PAIR, d.W * d.S, d.R * d.G * d.L, d.Q // d.L
     d.OFF_C = d.NB + d.AR * d.SA
-    d.EARLY = 1 + max(1, d.G // 4)
+    d.EARLY = 2
     ladder = {(-(-d.NB * f // 112), -(-d.NB * t // 112)) for f, t in LADDER}
     d.caps = tuple(sorted(ladder))
     d.sections = tuple(
@@ -372,8 +395,8 @@
     vmem = pl.BlockSpec(memory_space=VMEM)
     hbm = pl.BlockSpec(memory_space=HBM)
 
-    def shift(x, k):
-        return lax.ppermute(x, "col", [(c, (c + k) % G) for c in range(G)])
+    def move(x, pairs):
+        return lax.ppermute(x, "col", [(c, t) for c, t in pairs if 0 <= t < G])
 
     own = b_tiles.reshape(NB, T, T)
     pair_swap = [(r, r ^ (PAIR - 1)) for r in range(R)]
@@ -404,7 +427,9 @@
     sib = lax.ppermute(own, "row", pair_swap)
     spread = jnp.broadcast_to(group[None], (R * L, G, n_idx))
     a_from, spread = lax.optimization_barrier((a_own, spread))
-    a_early = [a_own] + [shift(a_from, k) for k in range(1, d.EARLY)]
+    up = move(a_from, [(c, c + 1) for c in range(G)])
+    down = move(a_from, [(c, c - 1) for c in range(G)])
+    a_early = [a_own, up, down]
     table = lax.all_to_all(spread, ("row", "layer"), 0, 0, tiled=True)
     table = table.reshape(R, L, G, n_idx).transpose(0, 2, 1, 3).reshape(d.N, n_idx)
 
@@ -418,7 +443,7 @@
             jax.ShapeDtypeStruct((YS, PAIR, NB), I32),
             jax.ShapeDtypeStruct((1,), I32),
         ],
-        scratch_shapes=[VMEM((Y, d.N, NB), I32)] * 2,
+        scratch_shapes=[VMEM((Y, d.N, NB), I32)] * 2 + [VMEM((YS * 4 * PAIR, NB), F32)],
         compiler_params=limit((2 * Y + 8, d.N, 128), (16, 256, 256)),
         name="plan",
     )(me, table, table)
@@ -432,7 +457,25 @@
         first, cap = caps
         two = cap > first
         second = max(cap - first, 1)
-        a_late = [shift(a_early[0], k) for k in range(d.EARLY, G)]
+        a_own, up, down = a_early
+        ends = move(a_own, [(0, G - 1), (G - 1, 0)])
+        a_slots = [
+            (a_own, [(0, 0, G)]),
+            (up, [(1, 1, G)]),
+            (down, [(1, 0, 1), (G - 1, 1, G - 1)]),
+            (ends, [(G - 1, 0, 1), (G - 1, G - 1, G)]),
+        ]
+        for k in range(2, G - 1):
+            back = G - k
+            if k == 2:
+                a_slots.append((move(up, [(c, c + 1) for c in range(1, G)]), [(k, k, G)]))
+            if back == 2:
+                a_slots.append((move(down, [(c, c - 1) for c in range(G - 1)]), [(k, 0, k)]))
+            direct = [(c, c + k) for c in range(G)] if k != 2 else []
+            direct += [(c, c - back) for c in range(G)] if back != 2 else []
+            if direct:
+                low, high = (k if back == 2 else 0), (k if k == 2 else G)
+                a_slots.append((move(a_own, direct), [(k, low, high)]))
         packs = pl.pallas_call(
             functools.partial(pack_kernel, d, first, cap),
             in_specs=[smem, smem, smem, hbm, hbm],
@@ -460,7 +503,6 @@
             return [rec, lax.ppermute(rec, "row", pair_swap)]
 
         received = [across(0), across(1) if two else [packs[1], packs[1]]]
-        a_list = list(a_early) + a_late
         src, aidx, oidx, starts = pl.pallas_call(
             functools.partial(list_kernel, d, first),
             in_specs=[smem, smem, smem],
@@ -478,11 +520,16 @@
             _, low, high, part = d.sections[k]
             b_local = [] if part == 1 else [own, sib]
             b_far = received[1 if part == 1 else 0]
-            a_part = a_list[low:high]
+            chosen = [
+                (x, tuple((use - low, c0, c1) for use, c0, c1 in uses if low <= use < high))
+                for x, uses in a_slots
+            ]
+            a_part = [x for x, uses in chosen if uses]
+            a_fill = tuple(uses for _, uses in chosen if uses)
             size = ((high - low) * d.AR * d.QL, T, T)
-            n_a = len(a_part) * d.AR * d.SA
+            n_a = (high - low) * d.AR * d.SA
             return pl.pallas_call(
-                functools.partial(product_kernel, d, k, depth, first, len(a_part), len(parts)),
+                functools.partial(product_kernel, d, k, depth, first, a_fill, len(parts)),
                 in_specs=[smem] * 5
                 + [hbm] * len(b_local)
                 + [vmem] * (2 + len(a_part) + len(parts)),
@@ -494,7 +541,7 @@
                     pltpu.SemaphoreType.DMA((depth,)),
                 ],
                 compiler_params=limit(
-                    (depth + 2 * n_a, T, T), size, *(x.shape for x in (*b_far, *parts))
+                    (depth + n_a + len(a_part) * d.AR * d.SA, T, T), size, *(x.shape for x in (*b_far, *parts))
                 ),
                 cost_estimate=pl.CostEstimate(
                     flops=5 * 10**9, bytes_accessed=10**6, transcendentals=0

time: 99.7 us -> 98.5 us (0.988)
  the two profiles are of different devices: /device:TPU:29 before, /device:TPU:0 now
where the time goes in v2:
time: 98.5 us; the launch traced here: 97.5 us
  waiting for transfers between devices  36.2 us (37%)
  Pallas kernels  29.6 us (30%)
  starting transfers between devices  16.6 us (17%)
  blocking collectives  12.4 us (13%)
  local copies, waits for them, and re-layouts  1.48 us (2%)
    ppermute x2, waiting for transfers between devices, across(): lax.ppermute(packed[k - 1:k], 'row', [(r, (r // PAIR + k) % Y * PAIR + r...  30.1 us
    pallas_call x4, Pallas kernels, products(): pl.pallas_call(functools.partial(product_kernel, d, k, depth, first, a_fi...  15.5 us
    all_gather x1, blocking collectives, on_device(): group = lax.all_gather(idx, 'col', axis=0, tiled=True)  12.4 us
    ppermute x5, starting transfers between devices, move(): return lax.ppermute(x, 'col', [(c, t) for c, t in pairs if 0 <= t < G])  9.75 us
    pallas_call x1, Pallas kernels, body(): pl.pallas_call(functools.partial(list_kernel, d, first), in_specs=[smem,...  7.1 us
    all_to_all x1, waiting for transfers between devices, on_device(): table = lax.all_to_all(spread, ('row', 'layer'), 0, 0, tiled=True)  4.68 us
    all_to_all x1, starting transfers between devices, on_device(): table = lax.all_to_all(spread, ('row', 'layer'), 0, 0, tiled=True)  3.74 us
    pallas_call x1, Pallas kernels, on_device(): pl.pallas_call(functools.partial(plan_kernel, d), in_specs=[smem, smem, v...  3.41 us
  transfers between devices with their start and end apart: 13, of which 5 were waited for; matrix products, arithmetic and copies ran while one was open for 1% of the time, Pallas kernels for 27%

profile of v2, /device:TPU:0, one launch (start us, length us, event | category | flops | bytes accessed | tf_op | source)
XLA Modules:
  0.0 97.5 jit_solution(8320460130852649959)
XLA Ops:
  0.5 1.4 %index.1 = s32[1,135]{1,0:T(1,128)} custom-call(s32[7,1,16]{2,1,0:T(1,128)} %bitcast.83, s32[1,1,7]{2,1,0:T(1,128)} %a_in.1, s32[4,1,4]{2,1,0:T(1,128)} %c_in.1), custom_call_target="tpu_custom_call" | custom-call | tf_op jit(solution)/shard_map/index/pallas_call | solution.py:412
  1.9 12.4 %all-gather = s32[4,1,135]{2,1,0:T(1,128)S(1)} all-gather(s32[1,1,135]{2,1,0:T(1,128)} %bitcast.82), channel_id=1, replica_groups=mesh['row'=4,'col'=4,'layer'=2] {'col'}, dimensions={0}, use_global_device_ids=true | all-gather | bytes 2700 | tf_op jit(solution)/shard_map/all_gather | solution.py:426
  14.3 0.6 broadcast_in_dim.2
  14.9 1.3 %collective-permute-start.81 = (f32[7,128,128]{2,1,0:T(8,128)}, f32[7,128,128]{2,1,0:T(8,128)S(1)}, u32[]{:S(2)}, u32[]{:S(2)}) collective-permute-start(f32[7,128,128]{2,1,0:T(8,128)} %bitcast.69), channel_id=1, source_target_pairs={{2,0},{4,2},{6,4},{3,1},{5,3},{7,5},{10,8},{12,10},{14,12},{11,9},... | collective-permute-start | bytes 1376264 | tf_op jit(solution)/shard_map/ppermute | solution.py:399
  16.2 4.6 %collective-permute-start.80 = (f32[7,128,128]{2,1,0:T(8,128)}, f32[7,128,128]{2,1,0:T(8,128)S(1)}, u32[]{:S(2)}, u32[]{:S(2)}) collective-permute-start(f32[7,128,128]{2,1,0:T(8,128)} %bitcast.70), channel_id=1, source_target_pairs={{0,2},{2,4},{4,6},{1,3},{3,5},{5,7},{8,10},{10,12},{12,14},{9,11},... | collective-permute-start | bytes 1376264 | tf_op jit(solution)/shard_map/ppermute | solution.py:399
  20.8 3.7 %all-to-all-start = ((s32[8,4,135]{2,1,0:T(4,128)}), s32[8,4,135]{2,1,0:T(4,128)S(1)}, u32[]{:S(2)}, u32[]{:S(2)}) async-start(s32[8,4,135]{2,1,0:T(4,128)} %broadcast_in_dim.2), calls=%async_computation | async-start | bytes 65536 | tf_op jit(solution)/shard_map/all_to_all | solution.py:433
  24.6 4.7 %all-to-all-done = s32[8,4,135]{2,1,0:T(4,128)S(1)} async-done(((s32[8,4,135]{2,1,0:T(4,128)}), s32[8,4,135]{2,1,0:T(4,128)S(1)}, u32[]{:S(2)}, u32[]{:S(2)}) %all-to-all-start) | async-done | bytes 17312 | tf_op jit(solution)/shard_map/all_to_all | solution.py:433
  29.4 3.4 %plan.1 = (s32[1,2,224]{2,1,0:T(2,128)S(1)}, s32[1,2]{1,0:T(1,128)S(1)}, s32[1,2,112]{2,1,0:T(2,128)S(1)}, s32[1]{0:T(128)}) custom-call(s32[3]{0:T(128)S(1)} %pad_add_fusion.me, s32[32,135]{1,0:T(8,128)S(1)} %reshape.46.gs.gv, s32[32,135]{1,0:T(8,128)S(1)} %reshape.46.gs.gv), custom_call_target="tpu_custom_call" | custom-call | tf_op jit(solution)/shard_map/plan/pallas_call | solution.py:436
  33.5 63.2 %conditional.1 = (f32[4,1,2,128,128]{4,3,2,1,0:T(8,128)S(1)}) conditional(s32[]{:T(128)} %bitcast.35, (s32[3]{0:T(128)S(1)}, s32[32,135]{1,0:T(8,128)S(1)}, s32[1,2,112]{2,1,0:T(2,128)S(1)}, s32[1,2,224]{2,1,0:T(2,128)S(1)}, s32[1,2]{1,0:T(1,128)S(1)}, /*index=5*/f32[112,128,128]{2,1,0:T(8,128)}, ...), branch_computations={%region_0.0_spmd, %region_1.0_spmd, %region_2.0_spmd, %region_3.0_... | conditional | flops 24999999488 | bytes 94277896 | solution.py:559
  33.7 2.1 %pack.13 = (f32[1,14,128,128]{3,2,1,0:T(8,128)S(1)}, f32[1,12,128,128]{3,2,1,0:T(8,128)S(1)}) custom-call(s32[3]{0:T(128)S(1)} %get-tuple-element.260.me, s32[1,2,224]{2,1,0:T(2,128)S(1)} %get-tuple-element.267.inv, s32[1,2]{1,0:T(1,128)S(1)} %get-tuple-element.268.cnt, f32[112,128,128]{2,1,0:T(8,128)} %get-tuple-element.269.own.refs_0_, ...), custom_call_target="tpu_custom_call" | custom-call | tf_op jit(solution)/shard_map/cond/branch_4_fun/pack/pallas_call | solution.py:479
  35.8 0.6 collective-permute-start.41
  36.5 21.8 %collective-permute-done.41.refs_2_ = f32[1,14,128,128]{3,2,1,0:T(8,128)S(1)} collective-permute-done((f32[1,14,128,128]{3,2,1,0:T(8,128)S(1)}, f32[1,14,128,128]{3,2,1,0:T(8,128)S(1)}, u32[]{:S(2)}, u32[]{:S(2)}) %collective-permute-start.41) | collective-permute-done | bytes 917536 | tf_op jit(solution)/shard_map/cond/branch_4_fun/ppermute | solution.py:495
  58.8 1.9 %collective-permute-start.38 = (f32[7,128,128]{2,1,0:T(8,128)S(1)}, f32[7,128,128]{2,1,0:T(8,128)S(1)}, u32[]{:S(2)}, u32[]{:S(2)}) collective-permute-start(f32[7,128,128]{2,1,0:T(8,128)S(1)} %copy-done.4), channel_id=1, source_target_pairs={{0,6},{6,0},{1,7},{7,1},{8,14},{14,8},{9,15},{15,9},{16,22},{22,16... | collective-permute-start | bytes 1376264 | tf_op jit(solution)/shard_map/cond/branch_4_fun/ppermute | solution.py:399
  60.7 0.7 collective-permute-start.39
  61.4 1.3 %collective-permute-start.40 = (f32[7,128,128]{2,1,0:T(8,128)S(1)}, f32[7,128,128]{2,1,0:T(8,128)S(1)}, u32[]{:S(2)}, u32[]{:S(2)}) collective-permute-start(f32[7,128,128]{2,1,0:T(8,128)S(1)} %get-tuple-element.274.refs_6_.refs_4_), channel_id=1, source_target_pairs={{2,0},{4,2},{3,1},{5,3},{10,8},{12,10},{11,9},{13,11},{18,16},{20,... | collective-permute-start | bytes 1376264 | tf_op jit(solution)/shard_map/cond/branch_4_fun/ppermute | solution.py:399
  62.8 7.1 %list.13 = (s32[112]{0:T(128)S(1)}, s32[112]{0:T(128)S(1)}, s32[112]{0:T(128)S(1)}, s32[5]{0:T(128)S(1)}) custom-call(s32[3]{0:T(128)S(1)} %get-tuple-element.260.me, s32[32,135]{1,0:T(8,128)S(1)} %get-tuple-element.261.gs, s32[1,2,112]{2,1,0:T(2,128)S(1)} %get-tuple-element.262.pos), custom_call_target="tpu_custom_call" | custom-call | flops 5000000000 | bytes 100000 | tf_op jit(solution)/shard_map/cond/branch_4_fun/list/pallas_call | solution.py:506
  69.9 8.3 %collective-permute-done.36.refs_0_ = f32[1,12,128,128]{3,2,1,0:T(8,128)S(1)} collective-permute-done((f32[1,12,128,128]{3,2,1,0:T(8,128)S(1)}, f32[1,12,128,128]{3,2,1,0:T(8,128)S(1)}, u32[]{:S(2)}, u32[]{:S(2)}) %collective-permute-start.36) | collective-permute-done | bytes 786464 | tf_op jit(solution)/shard_map/cond/branch_4_fun/ppermute | solution.py:495
  78.2 5.5 %products.53 = f32[4,128,128]{2,1,0:T(8,128)S(1)} custom-call(s32[3]{0:T(128)S(1)} %get-tuple-element.260.me, s32[112]{0:T(128)S(1)} %get-tuple-element.263.src, s32[112]{0:T(128)S(1)} %get-tuple-element.264.aidx, s32[112]{0:T(128)S(1)} %get-tuple-element.265.oidx, s32[5]{0:T(128)S(1)} %get-tuple-element.266.starts, f32[112,128,128]{2,1,0:T(8,128)S(1)} %bitcast.60, ...), custom_call_target="tpu_custom_call" | custom-call | flops 5000000000 | bytes 1000000 | tf_op jit(solution)/shard_map/cond/branch_4_fun/products/pallas_call | solution.py:531
  83.8 1.2 %collective-permute-done.40.refs_9_.refs_7_ = f32[7,128,128]{2,1,0:T(8,128)S(1)} collective-permute-done((f32[7,128,128]{2,1,0:T(8,128)S(1)}, f32[7,128,128]{2,1,0:T(8,128)S(1)}, u32[]{:S(2)}, u32[]{:S(2)}) %collective-permute-start.40) | collective-permute-done | bytes 458784 | tf_op jit(solution)/shard_map/cond/branch_4_fun/ppermute | solution.py:399
  85.0 2.4 %products.54 = f32[4,128,128]{2,1,0:T(8,128)S(1)} custom-call(s32[3]{0:T(128)S(1)} %get-tuple-element.260.me, s32[112]{0:T(128)S(1)} %get-tuple-element.263.src, s32[112]{0:T(128)S(1)} %get-tuple-element.264.aidx, s32[112]{0:T(128)S(1)} %get-tuple-element.265.oidx, s32[5]{0:T(128)S(1)} %get-tuple-element.266.starts, f32[112,128,128]{2,1,0:T(8,128)S(1)} %bitcast.60, ...), custom_call_target="tpu_custom_call" | custom-call | flops 5000000000 | bytes 1000000 | tf_op jit(solution)/shard_map/cond/branch_4_fun/products/pallas_call | solution.py:531
  87.4 1.3 %collective-permute-start.44 = (f32[4,128,128]{2,1,0:T(8,128)S(1)}, f32[4,128,128]{2,1,0:T(8,128)S(1)}, u32[]{:S(2)}, u32[]{:S(2)}) collective-permute-start(f32[4,128,128]{2,1,0:T(8,128)S(1)} %products.54), channel_id=1, source_target_pairs={{0,1},{1,0},{2,3},{3,2},{4,5},{5,4},{6,7},{7,6},{8,9},{9,8},{10,11... | collective-permute-start | bytes 786440 | tf_op jit(solution)/shard_map/cond/branch_4_fun/ppermute | solution.py:555
  88.8 6.8 %products.52.refs_8_ = f32[8,128,128]{2,1,0:T(8,128)S(1)} custom-call(s32[3]{0:T(128)S(1)} %get-tuple-element.260.me, s32[112]{0:T(128)S(1)} %get-tuple-element.263.src, s32[112]{0:T(128)S(1)} %get-tuple-element.264.aidx, s32[112]{0:T(128)S(1)} %get-tuple-element.265.oidx, s32[5]{0:T(128)S(1)} %get-tuple-element.266.starts, f32[112,128,128]{2,1,0:T(8,128)S(1)} %bitcast.60, ...), custom_call_target="tpu_custom_call" | custom-call | flops 5000000000 | bytes 1000000 | tf_op jit(solution)/shard_map/cond/branch_4_fun/products/pallas_call | solution.py:531
  95.9 0.8 products.55
  96.7 0.8 copy-done.9
  (26 shorter events, 1.6 us)
Async XLA Ops:
  0.0 33.5 %collective-permute-start.79 = (f32[112,128,128]{2,1,0:T(8,128)}, f32[112,128,128]{2,1,0:T(8,128)}, u32[]{:S(2)}, u32[]{:S(2)}) collective-permute-start(f32[112,128,128]{2,1,0:T(8,128)} %bitcast.41), channel_id=1, source_target_pairs={{0,8},{8,0},{16,24},{24,16},{1,9},{9,1},{17,25},{25,17},{2,10},{10... | collective-permute-start | bytes 22020104 | tf_op jit(solution)/shard_map/ppermute | solution.py:427
  14.9 18.5 %collective-permute-start.81 = (f32[7,128,128]{2,1,0:T(8,128)}, f32[7,128,128]{2,1,0:T(8,128)S(1)}, u32[]{:S(2)}, u32[]{:S(2)}) collective-permute-start(f32[7,128,128]{2,1,0:T(8,128)} %bitcast.69), channel_id=1, source_target_pairs={{2,0},{4,2},{6,4},{3,1},{5,3},{7,5},{10,8},{12,10},{14,12},{11,9},... | collective-permute-start | bytes 1376264 | tf_op jit(solution)/shard_map/ppermute | solution.py:399
  16.2 17.2 %collective-permute-start.80 = (f32[7,128,128]{2,1,0:T(8,128)}, f32[7,128,128]{2,1,0:T(8,128)S(1)}, u32[]{:S(2)}, u32[]{:S(2)}) collective-permute-start(f32[7,128,128]{2,1,0:T(8,128)} %bitcast.70), channel_id=1, source_target_pairs={{0,2},{2,4},{4,6},{1,3},{3,5},{5,7},{8,10},{10,12},{12,14},{9,11},... | collective-permute-start | bytes 1376264 | tf_op jit(solution)/shard_map/ppermute | solution.py:399
  20.8 8.5 %all-to-all-start = ((s32[8,4,135]{2,1,0:T(4,128)}), s32[8,4,135]{2,1,0:T(4,128)S(1)}, u32[]{:S(2)}, u32[]{:S(2)}) async-start(s32[8,4,135]{2,1,0:T(4,128)} %broadcast_in_dim.2), calls=%async_computation | async-start | bytes 65536 | tf_op jit(solution)/shard_map/all_to_all | solution.py:433
  33.7 25.2 %copy-start.4 = (f32[7,128,128]{2,1,0:T(8,128)S(1)}, f32[7,128,128]{2,1,0:T(8,128)}, u32[]{:S(2)}) copy-start(f32[7,128,128]{2,1,0:T(8,128)} %get-tuple-element.272.refs_4_.refs_2_) | copy-start | bytes 1376260 | tf_op jit(solution)/shard_map/cond
  33.7 44.5 %slice-start.8 = ((s8[7340032]{0:T(1024)(128)(4,1)}), s8[4194304]{0:T(1024)(128)(4,1)S(1)}, s32[]{:S(2)}) async-start(s8[7340032]{0:T(1024)(128)(4,1)} %bitcast.59), calls=%async_computation.9 | async-start | bytes 8388608 | tf_op jit(solution)/shard_map/cond
  35.8 22.4 %collective-permute-start.41 = (f32[1,14,128,128]{3,2,1,0:T(8,128)S(1)}, f32[1,14,128,128]{3,2,1,0:T(8,128)S(1)}, u32[]{:S(2)}, u32[]{:S(2)}) collective-permute-start(f32[1,14,128,128]{3,2,1,0:T(8,128)S(1)} %get-tuple-element.275), channel_id=1, source_target_pairs={{0,16},{8,24},{16,0},{24,8},{1,17},{9,25},{17,1},{25,9},{2,18},{10... | collective-permute-start | bytes 2752520 | tf_op jit(solution)/shard_map/cond/branch_4_fun/ppermute | solution.py:495
  58.2 20.0 %collective-permute-start.42 = (f32[1,14,128,128]{3,2,1,0:T(8,128)S(1)}, f32[1,14,128,128]{3,2,1,0:T(8,128)S(1)}, u32[]{:S(2)}, u32[]{:S(2)}) collective-permute-start(f32[1,14,128,128]{3,2,1,0:T(8,128)S(1)} %collective-permute-done.41.refs_2_), channel_id=1, source_target_pairs={{0,8},{8,0},{16,24},{24,16},{1,9},{9,1},{17,25},{25,17},{2,10},{10... | collective-permute-start | bytes 2752520 | tf_op jit(solution)/shard_map/cond/branch_4_fun/ppermute | solution.py:503
  58.2 20.0 %collective-permute-start.36 = (f32[1,12,128,128]{3,2,1,0:T(8,128)S(1)}, f32[1,12,128,128]{3,2,1,0:T(8,128)S(1)}, u32[]{:S(2)}, u32[]{:S(2)}) collective-permute-start(f32[1,12,128,128]{3,2,1,0:T(8,128)S(1)} %get-tuple-element.271), channel_id=1, source_target_pairs={{0,16},{8,24},{16,0},{24,8},{1,17},{9,25},{17,1},{25,9},{2,18},{10... | collective-permute-start | bytes 2359304 | tf_op jit(solution)/shard_map/cond/branch_4_fun/ppermute | solution.py:495
  58.8 25.0 %collective-permute-start.38 = (f32[7,128,128]{2,1,0:T(8,128)S(1)}, f32[7,128,128]{2,1,0:T(8,128)S(1)}, u32[]{:S(2)}, u32[]{:S(2)}) collective-permute-start(f32[7,128,128]{2,1,0:T(8,128)S(1)} %copy-done.4), channel_id=1, source_target_pairs={{0,6},{6,0},{1,7},{7,1},{8,14},{14,8},{9,15},{15,9},{16,22},{22,16... | collective-permute-start | bytes 1376264 | tf_op jit(solution)/shard_map/cond/branch_4_fun/ppermute | solution.py:399
  60.7 23.1 %collective-permute-start.39 = (f32[7,128,128]{2,1,0:T(8,128)S(1)}, f32[7,128,128]{2,1,0:T(8,128)S(1)}, u32[]{:S(2)}, u32[]{:S(2)}) collective-permute-start(f32[7,128,128]{2,1,0:T(8,128)S(1)} %get-tuple-element.273.refs_5_.refs_3_), channel_id=1, source_target_pairs={{2,4},{4,6},{3,5},{5,7},{10,12},{12,14},{11,13},{13,15},{18,20},{2... | collective-permute-start | bytes 1376264 | tf_op jit(solution)/shard_map/cond/branch_4_fun/ppermute | solution.py:399
  61.4 23.5 %collective-permute-start.40 = (f32[7,128,128]{2,1,0:T(8,128)S(1)}, f32[7,128,128]{2,1,0:T(8,128)S(1)}, u32[]{:S(2)}, u32[]{:S(2)}) collective-permute-start(f32[7,128,128]{2,1,0:T(8,128)S(1)} %get-tuple-element.274.refs_6_.refs_4_), channel_id=1, source_target_pairs={{2,0},{4,2},{3,1},{5,3},{10,8},{12,10},{11,9},{13,11},{18,16},{20,... | collective-permute-start | bytes 1376264 | tf_op jit(solution)/shard_map/cond/branch_4_fun/ppermute | solution.py:399
  62.7 15.5 %slice-start.9 = ((s8[7340032]{0:T(1024)(128)(4,1)}), s8[3145728]{0:T(1024)(128)(4,1)S(1)}, s32[]{:S(2)}) async-start(s8[7340032]{0:T(1024)(128)(4,1)} %bitcast.59), calls=%async_computation.10 | async-start | bytes 6291456 | tf_op jit(solution)/shard_map/cond
  78.2 17.4 %collective-permute-start.37 = (f32[1,12,128,128]{3,2,1,0:T(8,128)S(1)}, f32[1,12,128,128]{3,2,1,0:T(8,128)S(1)}, u32[]{:S(2)}, u32[]{:S(2)}) collective-permute-start(f32[1,12,128,128]{3,2,1,0:T(8,128)S(1)} %collective-permute-done.36.refs_0_), channel_id=1, source_target_pairs={{0,8},{8,0},{16,24},{24,16},{1,9},{9,1},{17,25},{25,17},{2,10},{10... | collective-permute-start | bytes 2359304 | tf_op jit(solution)/shard_map/cond/branch_4_fun/ppermute | solution.py:503
  83.7 11.9 %collective-permute-start.43 = (f32[4,128,128]{2,1,0:T(8,128)S(1)}, f32[4,128,128]{2,1,0:T(8,128)S(1)}, u32[]{:S(2)}, u32[]{:S(2)}) collective-permute-start(f32[4,128,128]{2,1,0:T(8,128)S(1)} %products.53), channel_id=1, source_target_pairs={{0,1},{1,0},{2,3},{3,2},{4,5},{5,4},{6,7},{7,6},{8,9},{9,8},{10,11... | collective-permute-start | bytes 786440 | tf_op jit(solution)/shard_map/cond/branch_4_fun/ppermute | solution.py:555
  87.4 8.4 %collective-permute-start.44 = (f32[4,128,128]{2,1,0:T(8,128)S(1)}, f32[4,128,128]{2,1,0:T(8,128)S(1)}, u32[]{:S(2)}, u32[]{:S(2)}) collective-permute-start(f32[4,128,128]{2,1,0:T(8,128)S(1)} %products.54), channel_id=1, source_target_pairs={{0,1},{1,0},{2,3},{3,2},{4,5},{5,4},{6,7},{7,6},{8,9},{9,8},{10,11... | collective-permute-start | bytes 786440 | tf_op jit(solution)/shard_map/cond/branch_4_fun/ppermute | solution.py:555
  96.7 0.8 copy-start.9

commit v3 on v1

--- a/solution.py
+++ b/solution.py
@@ -432,7 +432,11 @@
         first, cap = caps
         two = cap > first
         second = max(cap - first, 1)
-        a_late = [shift(a_early[0], k) for k in range(d.EARLY, G)]
+        e = d.EARLY - 1
+        a_late = [
+            shift(a_early[e], k - e) if k - e < G - k else shift(a_early[0], k)
+            for k in range(d.EARLY, G)
+        ]
         packs = pl.pallas_call(
             functools.partial(pack_kernel, d, first, cap),
             in_specs=[smem, smem, smem, hbm, hbm],

time: 99.7 us -> 91.7 us (0.920)
  the two profiles are of different devices: /device:TPU:29 before, /device:TPU:0 now
where the time goes in v3:
time: 91.7 us; the launch traced here: 91.4 us
  waiting for transfers between devices  36.6 us (40%)
  Pallas kernels  28.9 us (32%)
  blocking collectives  12.4 us (14%)
  starting transfers between devices  10.8 us (12%)
  local copies, waits for them, and re-layouts  1.47 us (2%)
    ppermute x2, waiting for transfers between devices, across(): lax.ppermute(packed[k - 1:k], 'row', [(r, (r // PAIR + k) % Y * PAIR + r...  29.3 us
    pallas_call x4, Pallas kernels, products(): pl.pallas_call(functools.partial(product_kernel, d, k, depth, first, len(...  15 us
    all_gather x1, blocking collectives, on_device(): group = lax.all_gather(idx, 'col', axis=0, tiled=True)  12.4 us
    pallas_call x1, Pallas kernels, body(): pl.pallas_call(functools.partial(list_kernel, d, first), in_specs=[smem,...  7.02 us
    all_to_all x1, waiting for transfers between devices, on_device(): table = lax.all_to_all(spread, ('row', 'layer'), 0, 0, tiled=True)  4.68 us
    ppermute x3, starting transfers between devices, shift(): return lax.ppermute(x, 'col', [(c, (c + k) % G) for c in range(G)])  3.76 us
    all_to_all x1, starting transfers between devices, on_device(): table = lax.all_to_all(spread, ('row', 'layer'), 0, 0, tiled=True)  3.72 us
    pallas_call x1, Pallas kernels, on_device(): pl.pallas_call(functools.partial(plan_kernel, d), in_specs=[smem, smem, v...  3.38 us
  transfers between devices with their start and end apart: 11, of which 6 were waited for; matrix products, arithmetic and copies ran while one was open for 1% of the time, Pallas kernels for 29%

profile of v3, /device:TPU:0, one launch (start us, length us, event | category | flops | bytes accessed | tf_op | source)
XLA Modules:
  0.0 91.4 jit_solution(2982681517783519817)
XLA Ops:
  0.0 0.5 collective-permute-start.70
  0.5 1.4 %index.1 = s32[1,135]{1,0:T(1,128)} custom-call(s32[7,1,16]{2,1,0:T(1,128)} %bitcast.82, s32[1,1,7]{2,1,0:T(1,128)} %a_in.1, s32[4,1,4]{2,1,0:T(1,128)} %c_in.1), custom_call_target="tpu_custom_call" | custom-call | tf_op jit(solution)/shard_map/index/pallas_call | solution.py:389
  1.9 12.4 %all-gather = s32[4,1,135]{2,1,0:T(1,128)S(1)} all-gather(s32[1,1,135]{2,1,0:T(1,128)} %bitcast.81), channel_id=1, replica_groups=mesh['row'=4,'col'=4,'layer'=2] {'col'}, dimensions={0}, use_global_device_ids=true | all-gather | bytes 2700 | tf_op jit(solution)/shard_map/all_gather | solution.py:403
  14.3 0.6 broadcast_in_dim.2
  15.0 3.7 %all-to-all-start = ((s32[8,4,135]{2,1,0:T(4,128)}), s32[8,4,135]{2,1,0:T(4,128)S(1)}, u32[]{:S(2)}, u32[]{:S(2)}) async-start(s32[8,4,135]{2,1,0:T(4,128)} %broadcast_in_dim.2), calls=%async_computation | async-start | bytes 65536 | tf_op jit(solution)/shard_map/all_to_all | solution.py:408
  18.8 4.7 %all-to-all-done = s32[8,4,135]{2,1,0:T(4,128)S(1)} async-done(((s32[8,4,135]{2,1,0:T(4,128)}), s32[8,4,135]{2,1,0:T(4,128)S(1)}, u32[]{:S(2)}, u32[]{:S(2)}) %all-to-all-start) | async-done | bytes 17312 | tf_op jit(solution)/shard_map/all_to_all | solution.py:408
  23.5 3.4 %plan.1 = (s32[1,2,224]{2,1,0:T(2,128)S(1)}, s32[1,2]{1,0:T(1,128)S(1)}, s32[1,2,112]{2,1,0:T(2,128)S(1)}, s32[1]{0:T(128)}) custom-call(s32[3]{0:T(128)S(1)} %pad_add_fusion.me, s32[32,135]{1,0:T(8,128)S(1)} %reshape.46.gs.gv, s32[32,135]{1,0:T(8,128)S(1)} %reshape.46.gs.gv), custom_call_target="tpu_custom_call" | custom-call | tf_op jit(solution)/shard_map/plan/pallas_call | solution.py:411
  27.5 0.3 collective-permute-done.71
  27.9 62.7 %conditional.1 = (f32[4,1,2,128,128]{4,3,2,1,0:T(8,128)S(1)}) conditional(s32[]{:T(128)} %bitcast.35, (s32[3]{0:T(128)S(1)}, s32[32,135]{1,0:T(8,128)S(1)}, s32[1,2,112]{2,1,0:T(2,128)S(1)}, s32[1,2,224]{2,1,0:T(2,128)S(1)}, s32[1,2]{1,0:T(1,128)S(1)}, /*index=5*/f32[112,128,128]{2,1,0:T(8,128)}, ...), branch_computations={%region_0.0_spmd, %region_1.0_spmd, %region_2.0_spmd, %region_3.0_... | conditional | flops 24999999488 | bytes 92442856 | solution.py:516
  27.9 2.1 %pack.13 = (f32[1,14,128,128]{3,2,1,0:T(8,128)S(1)}, f32[1,12,128,128]{3,2,1,0:T(8,128)S(1)}) custom-call(s32[3]{0:T(128)S(1)} %get-tuple-element.238.me, s32[1,2,224]{2,1,0:T(2,128)S(1)} %get-tuple-element.245.inv, s32[1,2]{1,0:T(1,128)S(1)} %get-tuple-element.246.cnt, f32[112,128,128]{2,1,0:T(8,128)} %get-tuple-element.247.own.refs_0_, ...), custom_call_target="tpu_custom_call" | custom-call | tf_op jit(solution)/shard_map/cond/branch_4_fun/pack/pallas_call | solution.py:440
  30.0 1.6 %collective-permute-start.36 = (f32[1,14,128,128]{3,2,1,0:T(8,128)S(1)}, f32[1,14,128,128]{3,2,1,0:T(8,128)S(1)}, u32[]{:S(2)}, u32[]{:S(2)}) collective-permute-start(f32[1,14,128,128]{3,2,1,0:T(8,128)S(1)} %get-tuple-element.252), channel_id=1, source_target_pairs={{0,16},{8,24},{16,0},{24,8},{1,17},{9,25},{17,1},{25,9},{2,18},{10... | collective-permute-start | bytes 2752520 | tf_op jit(solution)/shard_map/cond/branch_4_fun/ppermute | solution.py:456
  31.6 20.8 %collective-permute-done.36.refs_2_ = f32[1,14,128,128]{3,2,1,0:T(8,128)S(1)} collective-permute-done((f32[1,14,128,128]{3,2,1,0:T(8,128)S(1)}, f32[1,14,128,128]{3,2,1,0:T(8,128)S(1)}, u32[]{:S(2)}, u32[]{:S(2)}) %collective-permute-start.36) | collective-permute-done | bytes 917536 | tf_op jit(solution)/shard_map/cond/branch_4_fun/ppermute | solution.py:456
  52.4 0.6 collective-permute-start.32
  53.0 3.8 %collective-permute-start.35 = (f32[7,128,128]{2,1,0:T(8,128)S(1)}, f32[7,128,128]{2,1,0:T(8,128)S(1)}, u32[]{:S(2)}, u32[]{:S(2)}) collective-permute-start(f32[7,128,128]{2,1,0:T(8,128)S(1)} %copy-done.4), channel_id=1, source_target_pairs={{0,6},{2,0},{4,2},{6,4},{1,7},{3,1},{5,3},{7,5},{8,14},{10,8},{12,... | collective-permute-start | bytes 1376264 | tf_op jit(solution)/shard_map/cond/branch_4_fun/ppermute | solution.py:376
  56.8 7.0 %list.13 = (s32[112]{0:T(128)S(1)}, s32[112]{0:T(128)S(1)}, s32[112]{0:T(128)S(1)}, s32[5]{0:T(128)S(1)}) custom-call(s32[3]{0:T(128)S(1)} %get-tuple-element.238.me, s32[32,135]{1,0:T(8,128)S(1)} %get-tuple-element.239.gs, s32[1,2,112]{2,1,0:T(2,128)S(1)} %get-tuple-element.240.pos), custom_call_target="tpu_custom_call" | custom-call | flops 5000000000 | bytes 100000 | tf_op jit(solution)/shard_map/cond/branch_4_fun/list/pallas_call | solution.py:468
  63.8 8.5 %collective-permute-done.32.refs_0_ = f32[1,12,128,128]{3,2,1,0:T(8,128)S(1)} collective-permute-done((f32[1,12,128,128]{3,2,1,0:T(8,128)S(1)}, f32[1,12,128,128]{3,2,1,0:T(8,128)S(1)}, u32[]{:S(2)}, u32[]{:S(2)}) %collective-permute-start.32) | collective-permute-done | bytes 786464 | tf_op jit(solution)/shard_map/cond/branch_4_fun/ppermute | solution.py:456
  72.4 3.8 %products.53 = f32[4,128,128]{2,1,0:T(8,128)S(1)} custom-call(s32[3]{0:T(128)S(1)} %get-tuple-element.238.me, s32[112]{0:T(128)S(1)} %get-tuple-element.241.src, s32[112]{0:T(128)S(1)} %get-tuple-element.242.aidx, s32[112]{0:T(128)S(1)} %get-tuple-element.243.oidx, s32[5]{0:T(128)S(1)} %get-tuple-element.244.starts, f32[112,128,128]{2,1,0:T(8,128)S(1)} %bitcast.60, ...), custom_call_target="tpu_custom_call" | custom-call | flops 5000000000 | bytes 1000000 | tf_op jit(solution)/shard_map/cond/branch_4_fun/products/pallas_call | solution.py:488
  76.2 0.6 collective-permute-start.38
  76.7 0.8 collective-permute-done.34.refs_6_.refs_4_
  77.5 3.7 %products.54 = f32[4,128,128]{2,1,0:T(8,128)S(1)} custom-call(s32[3]{0:T(128)S(1)} %get-tuple-element.238.me, s32[112]{0:T(128)S(1)} %get-tuple-element.241.src, s32[112]{0:T(128)S(1)} %get-tuple-element.242.aidx, s32[112]{0:T(128)S(1)} %get-tuple-element.243.oidx, s32[5]{0:T(128)S(1)} %get-tuple-element.244.starts, f32[112,128,128]{2,1,0:T(8,128)S(1)} %bitcast.60, ...), custom_call_target="tpu_custom_call" | custom-call | flops 5000000000 | bytes 1000000 | tf_op jit(solution)/shard_map/cond/branch_4_fun/products/pallas_call | solution.py:488
  81.3 6.8 %products.52.refs_6_ = f32[8,128,128]{2,1,0:T(8,128)S(1)} custom-call(s32[3]{0:T(128)S(1)} %get-tuple-element.238.me, s32[112]{0:T(128)S(1)} %get-tuple-element.241.src, s32[112]{0:T(128)S(1)} %get-tuple-element.242.aidx, s32[112]{0:T(128)S(1)} %get-tuple-element.243.oidx, s32[5]{0:T(128)S(1)} %get-tuple-element.244.starts, f32[112,128,128]{2,1,0:T(8,128)S(1)} %bitcast.60, ...), custom_call_target="tpu_custom_call" | custom-call | flops 5000000000 | bytes 1000000 | tf_op jit(solution)/shard_map/cond/branch_4_fun/products/pallas_call | solution.py:488
  88.1 1.5 %collective-permute-done.39.refs_8_ = f32[4,128,128]{2,1,0:T(8,128)S(1)} collective-permute-done((f32[4,128,128]{2,1,0:T(8,128)S(1)}, f32[4,128,128]{2,1,0:T(8,128)S(1)}, u32[]{:S(2)}, u32[]{:S(2)}) %collective-permute-start.39) | collective-permute-done | bytes 262176 | tf_op jit(solution)/shard_map/cond/branch_4_fun/ppermute | solution.py:512
  89.6 0.7 products.55
  90.6 0.8 copy-done.9
  (22 shorter events, 0.2 us)
Async XLA Ops:
  0.0 27.9 %collective-permute-start.70 = (f32[112,128,128]{2,1,0:T(8,128)}, f32[112,128,128]{2,1,0:T(8,128)}, u32[]{:S(2)}, u32[]{:S(2)}) collective-permute-start(f32[112,128,128]{2,1,0:T(8,128)} %bitcast.41), channel_id=1, source_target_pairs={{0,8},{8,0},{16,24},{24,16},{1,9},{9,1},{17,25},{25,17},{2,10},{10... | collective-permute-start | bytes 22020104 | tf_op jit(solution)/shard_map/ppermute | solution.py:404
  14.9 12.9 %collective-permute-start.71 = (f32[7,128,128]{2,1,0:T(8,128)}, f32[7,128,128]{2,1,0:T(8,128)S(1)}, u32[]{:S(2)}, u32[]{:S(2)}) collective-permute-start(f32[7,128,128]{2,1,0:T(8,128)} %bitcast.69), channel_id=1, source_target_pairs={{0,2},{2,4},{4,6},{6,0},{1,3},{3,5},{5,7},{7,1},{8,10},{10,12},{12... | collective-permute-start | bytes 1376264 | tf_op jit(solution)/shard_map/ppermute | solution.py:376
  15.0 8.5 %all-to-all-start = ((s32[8,4,135]{2,1,0:T(4,128)}), s32[8,4,135]{2,1,0:T(4,128)S(1)}, u32[]{:S(2)}, u32[]{:S(2)}) async-start(s32[8,4,135]{2,1,0:T(4,128)} %broadcast_in_dim.2), calls=%async_computation | async-start | bytes 65536 | tf_op jit(solution)/shard_map/all_to_all | solution.py:408
  27.9 25.1 %copy-start.4 = (f32[7,128,128]{2,1,0:T(8,128)S(1)}, f32[7,128,128]{2,1,0:T(8,128)}, u32[]{:S(2)}) copy-start(f32[7,128,128]{2,1,0:T(8,128)} %get-tuple-element.250.refs_4_.refs_2_) | copy-start | bytes 1376260 | tf_op jit(solution)/shard_map/cond
  27.9 44.5 %slice-start.8 = ((s8[7340032]{0:T(1024)(128)(4,1)}), s8[4194304]{0:T(1024)(128)(4,1)S(1)}, s32[]{:S(2)}) async-start(s8[7340032]{0:T(1024)(128)(4,1)} %bitcast.59), calls=%async_computation.9 | async-start | bytes 8388608 | tf_op jit(solution)/shard_map/cond
  30.0 22.4 %collective-permute-start.36 = (f32[1,14,128,128]{3,2,1,0:T(8,128)S(1)}, f32[1,14,128,128]{3,2,1,0:T(8,128)S(1)}, u32[]{:S(2)}, u32[]{:S(2)}) collective-permute-start(f32[1,14,128,128]{3,2,1,0:T(8,128)S(1)} %get-tuple-element.252), channel_id=1, source_target_pairs={{0,16},{8,24},{16,0},{24,8},{1,17},{9,25},{17,1},{25,9},{2,18},{10... | collective-permute-start | bytes 2752520 | tf_op jit(solution)/shard_map/cond/branch_4_fun/ppermute | solution.py:456
  52.4 20.0 %collective-permute-start.37 = (f32[1,14,128,128]{3,2,1,0:T(8,128)S(1)}, f32[1,14,128,128]{3,2,1,0:T(8,128)S(1)}, u32[]{:S(2)}, u32[]{:S(2)}) collective-permute-start(f32[1,14,128,128]{3,2,1,0:T(8,128)S(1)} %collective-permute-done.36.refs_2_), channel_id=1, source_target_pairs={{0,8},{8,0},{16,24},{24,16},{1,9},{9,1},{17,25},{25,17},{2,10},{10... | collective-permute-start | bytes 2752520 | tf_op jit(solution)/shard_map/cond/branch_4_fun/ppermute | solution.py:464
  52.4 20.0 %collective-permute-start.32 = (f32[1,12,128,128]{3,2,1,0:T(8,128)S(1)}, f32[1,12,128,128]{3,2,1,0:T(8,128)S(1)}, u32[]{:S(2)}, u32[]{:S(2)}) collective-permute-start(f32[1,12,128,128]{3,2,1,0:T(8,128)S(1)} %get-tuple-element.249), channel_id=1, source_target_pairs={{0,16},{8,24},{16,0},{24,8},{1,17},{9,25},{17,1},{25,9},{2,18},{10... | collective-permute-start | bytes 2359304 | tf_op jit(solution)/shard_map/cond/branch_4_fun/ppermute | solution.py:456
  53.0 23.7 %collective-permute-start.35 = (f32[7,128,128]{2,1,0:T(8,128)S(1)}, f32[7,128,128]{2,1,0:T(8,128)S(1)}, u32[]{:S(2)}, u32[]{:S(2)}) collective-permute-start(f32[7,128,128]{2,1,0:T(8,128)S(1)} %copy-done.4), channel_id=1, source_target_pairs={{0,6},{2,0},{4,2},{6,4},{1,7},{3,1},{5,3},{7,5},{8,14},{10,8},{12,... | collective-permute-start | bytes 1376264 | tf_op jit(solution)/shard_map/cond/branch_4_fun/ppermute | solution.py:376
  56.8 20.7 %collective-permute-start.34 = (f32[7,128,128]{2,1,0:T(8,128)S(1)}, f32[7,128,128]{2,1,0:T(8,128)S(1)}, u32[]{:S(2)}, u32[]{:S(2)}) collective-permute-start(f32[7,128,128]{2,1,0:T(8,128)S(1)} %get-tuple-element.251.refs_5_.refs_3_), channel_id=1, source_target_pairs={{0,2},{2,4},{4,6},{6,0},{1,3},{3,5},{5,7},{7,1},{8,10},{10,12},{12... | collective-permute-start | bytes 1376264 | tf_op jit(solution)/shard_map/cond/branch_4_fun/ppermute | solution.py:376
  56.8 15.6 %slice-start.9 = ((s8[7340032]{0:T(1024)(128)(4,1)}), s8[3145728]{0:T(1024)(128)(4,1)S(1)}, s32[]{:S(2)}) async-start(s8[7340032]{0:T(1024)(128)(4,1)} %bitcast.59), calls=%async_computation.10 | async-start | bytes 6291456 | tf_op jit(solution)/shard_map/cond
  72.3 15.7 %collective-permute-start.33 = (f32[1,12,128,128]{3,2,1,0:T(8,128)S(1)}, f32[1,12,128,128]{3,2,1,0:T(8,128)S(1)}, u32[]{:S(2)}, u32[]{:S(2)}) collective-permute-start(f32[1,12,128,128]{3,2,1,0:T(8,128)S(1)} %collective-permute-done.32.refs_0_), channel_id=1, source_target_pairs={{0,8},{8,0},{16,24},{24,16},{1,9},{9,1},{17,25},{25,17},{2,10},{10... | collective-permute-start | bytes 2359304 | tf_op jit(solution)/shard_map/cond/branch_4_fun/ppermute | solution.py:464
  76.2 11.9 %collective-permute-start.38 = (f32[4,128,128]{2,1,0:T(8,128)S(1)}, f32[4,128,128]{2,1,0:T(8,128)S(1)}, u32[]{:S(2)}, u32[]{:S(2)}) collective-permute-start(f32[4,128,128]{2,1,0:T(8,128)S(1)} %products.53), channel_id=1, source_target_pairs={{0,1},{1,0},{2,3},{3,2},{4,5},{5,4},{6,7},{7,6},{8,9},{9,8},{10,11... | collective-permute-start | bytes 786440 | tf_op jit(solution)/shard_map/cond/branch_4_fun/ppermute | solution.py:512
  81.2 8.4 %collective-permute-start.39 = (f32[4,128,128]{2,1,0:T(8,128)S(1)}, f32[4,128,128]{2,1,0:T(8,128)S(1)}, u32[]{:S(2)}, u32[]{:S(2)}) collective-permute-start(f32[4,128,128]{2,1,0:T(8,128)S(1)} %products.54), channel_id=1, source_target_pairs={{0,1},{1,0},{2,3},{3,2},{4,5},{5,4},{6,7},{7,6},{8,9},{9,8},{10,11... | collective-permute-start | bytes 786440 | tf_op jit(solution)/shard_map/cond/branch_4_fun/ppermute | solution.py:512
  90.6 0.8 copy-start.9
